TPU v7x, 256 devices: a 4x2x16 block of a 4x16x16 slice. The times are simulated.
256 devices in a mesh: parts: 2 (over y), samp: 128 (over z, x, core).
Axes of the slice: x: 4, y: 2, z: 16, core: 2. Of those that a mesh axis runs over, the one named last changes fastest.
The devices are a block of a 4x16x16 slice.
Arguments:
- expression: bfloat16 [8192, 20480], P(('parts', 'samp')), parts along dimension 0, may hold values from -24 to 24
- current: bfloat16 [8192, 256], P(('parts', 'samp')), parts along dimension 0, may hold values from -6 to 6
- next_packed: int32 [512, 256], P(('parts', 'samp')), parts along dimension 0, may hold values from -2147483648 to 1789569706, as said below
- covariates: float32 [8192, 64], P(('parts', 'samp')), parts along dimension 0, may hold values from -1 to 1
Outputs:
- scores: float32 [40960, 256], P(('parts', 'samp')), parts along dimension 0
- next_block: bfloat16 [8192, 256], P(('parts', 'samp')), parts along dimension 0
There are 2 independent parts, one for each index of `parts`. A program takes and returns all parts, laid end to end along the dimension named above; each array names one. Nothing has to cross between parts.
Inputs may be any that keep to these rules, and one draw needn't show every extreme that they name: Each word holds the dosages (0, 1 or 2) of 16 consecutive samples of one variant, two bits a sample: sample 16 w + j of variant v in bits 2 j and 2 j + 1 of next_packed[v, w], bit 31 being the sign bit of the int32 word.
All inputs are finite; a program needn't handle non-finite values.
Results may differ from a plain program's by a relative error of at most 0.0004.
Values may be sent and summed in bfloat16 or wider, within the bound.
No kernel may reach another device: no remote copies, remote signals or barrier semaphores. Data moves between devices by JAX's collectives and lax.ppermute only.
A program may use at most 64 MiB of HBM per device.

v0:
```python
import functools

import jax
import jax.numpy as jnp
from jax import lax
from jax.experimental import pallas as pl
from jax.experimental.pallas import tpu as pltpu
from jax.sharding import Mesh
from jax.sharding import PartitionSpec as P

RING = 8
LOCAL = 16
SPEC = P(("parts", "q", "j"), None)
F32 = jnp.float32
BF16 = jnp.bfloat16
HIGHEST = lax.Precision.HIGHEST
WORD = 16


def dot(left, right, dims, precision=None):
    return lax.dot_general(
        left, right, (dims, ((), ())), precision=precision, preferred_element_type=F32
    )


def prepare_kernel(expression_ref, current_ref, covariates_ref, packed_ref, out_ref, words_ref):
    rows, genes = expression_ref.shape
    share = genes // (RING * LOCAL)
    cov = covariates_ref[...]
    high = cov.astype(BF16)
    low = (cov - high.astype(F32)).astype(BF16)
    own = [current_ref[...], high, low]
    for j in range(LOCAL):
        pieces = []
        for q in range(RING):
            at = (q * LOCAL + j) * share
            pieces.append(expression_ref[:, at : at + share])
        out_ref[j * rows : (j + 1) * rows, :] = jnp.concatenate(pieces + own, axis=1)
    held, words = packed_ref.shape
    split = words // RING
    words_ref[...] = jnp.zeros_like(words_ref)
    packed = packed_ref[...]
    for q in range(RING):
        words_ref[q * 8 : q * 8 + held, 0:split] = packed[:, q * split : (q + 1) * split]


def product_kernel(genes, variants, where_ref, rows_ref, *refs):
    outs, whole_ref = refs[:-1], refs[-1]
    whole_ref[...] = dot(rows_ref[:, :genes], rows_ref[:, genes : genes + variants], ((0,), (0,)))
    share = genes // RING
    half = share // 2
    for ahead in range(RING):
        at = lax.rem(where_ref[1] + ahead, RING) * share
        for part in range(2):
            outs[2 * ahead + part][...] = whole_ref[pl.ds(at + part * half, half), :]


def total_kernel(scale, *refs):
    out_ref = refs[-1]
    half = refs[0].shape[0]
    for part in range(2):
        terms = [ref[...] for ref in refs[part:-1:2]]
        out_ref[part * half : (part + 1) * half, :] = sum(terms[1:], terms[0]) * scale


def unpack(position, word_refs, held, share):
    words = jnp.concatenate([ref[0:held, 0:share] for ref in word_refs], axis=0)
    wide = jnp.concatenate([words] * 4, axis=1)
    lane = lax.broadcasted_iota(jnp.int32, wide.shape, 1)
    octets = (lax.shift_right_logical(wide, 8 * (lane // share)) & 255).astype(F32).astype(BF16)
    count = RING * held
    row = lax.broadcasted_iota(jnp.int32, (count, count), 0)
    col = lax.broadcasted_iota(jnp.int32, (count, count), 1)
    behind = (position + RING - row // held) % RING
    order = (col // held == behind) & (col % held == row % held)
    octets = dot(order.astype(F32).astype(BF16), octets, ((1,), (0,))).astype(BF16)
    samples = share * WORD
    row = lax.broadcasted_iota(jnp.int32, (4 * share, samples), 0)
    col = lax.broadcasted_iota(jnp.int32, (4 * share, samples), 1)
    pick = (row % share == col // WORD) & (row // share == (col % WORD) // 4)
    spread = dot(octets, pick.astype(F32).astype(BF16), ((1,), (0,))).astype(jnp.int32)
    place = lax.broadcasted_iota(jnp.int32, spread.shape, 1)
    return (lax.shift_right_logical(spread, 2 * (place % 4)) & 3).astype(F32)


def covariate_terms(rows_ref, at, covs):
    return [rows_ref[:, at + k * covs : at + (k + 1) * covs] for k in range(2)]


def stats_kernel(held, share, at, covs, where_ref, rows_ref, *refs):
    out_ref = refs[RING]
    dosage = unpack(where_ref[1], refs[:RING], held, share)
    count, samples = dosage.shape
    ones = jnp.ones((8, samples), F32)
    wide = jnp.concatenate([dosage, ones], axis=0)
    exact = wide.astype(BF16)
    terms = covariate_terms(rows_ref, at, covs)
    projected = sum(dot(exact, term, ((1,), (0,))) for term in reversed(terms))
    half = covs // 2
    height = count + 8 + half
    cov = sum(term.astype(F32) for term in reversed(terms))
    gram = dot(cov, cov, ((0,), (0,)), HIGHEST)
    counted = jnp.sum(wide, axis=1, keepdims=True)
    squares = jnp.sum(wide * wide, axis=1, keepdims=True)
    pad = jnp.zeros((count + 8, covs - 2), F32)
    table = jnp.concatenate([projected, counted, squares, pad], axis=1)
    lower = jnp.concatenate([gram[0:half], gram[half:]], axis=1)
    out_ref[0 : count + 8, :] = table
    out_ref[count + 8 : height, :] = lower


def finish_kernel(held, share, at, variants, covs, total, where_ref, rows_ref, *refs):
    out_ref = refs[2 * RING]
    dosage = unpack(where_ref[1], refs[:RING], held, share)
    count, _ = dosage.shape
    half = covs // 2
    table = refs[RING][...]
    for ref in refs[RING + 1 : 2 * RING]:
        table = table + ref[...]
    gram = jnp.concatenate(
        [
            table[count + 8 : count + 8 + half, 0:covs],
            table[count + 8 : count + 8 + half, covs : 2 * covs],
        ],
        axis=0,
    )
    projected = table[0:count, 0:covs]
    cov_sums = table[count : count + 1, 0:covs]
    counted = table[0:count, covs : covs + 1]
    squares = table[0:count, covs + 1 : covs + 2]
    average = counted / total
    loading = projected - average * cov_sums
    through = dot(loading, gram, ((1,), (0,)), HIGHEST)
    sq_norm = (
        squares
        - counted * average
        + jnp.sum(loading * (through - 2.0 * loading), axis=1, keepdims=True)
    )
    cov = sum(term.astype(F32) for term in reversed(covariate_terms(rows_ref, at, covs)))
    leftover = dosage - average - dot(loading, cov, ((1,), (1,)), HIGHEST)
    scaled = (leftover * lax.rsqrt(sq_norm / total + 1e-05)).astype(BF16)
    row = lax.broadcasted_iota(jnp.int32, (count, variants), 0)
    col = lax.broadcasted_iota(jnp.int32, (count, variants), 1)
    target = (row // held) * (held * LOCAL) + where_ref[0] * held + row % held
    place = (col == target).astype(F32).astype(BF16)
    out_ref[...] = dot(scaled, place, ((0,), (0,))).astype(BF16)


def exchange(array, axis):
    return lax.all_to_all(array, axis, split_axis=0, concat_axis=0, tiled=True)


def shift(array, by):
    return lax.ppermute(array, "q", [(k, (k + by) % RING) for k in range(RING)])


def kernel(body, out_shape, given=(), scratch=()):
    specs = [pl.BlockSpec(memory_space=space) for space in given]

    def call(*operands):
        rest = operands[len(specs) :]
        held = [pltpu.with_memory_space_constraint(array, pltpu.VMEM) for array in rest]
        return pl.pallas_call(
            body,
            out_shape=out_shape,
            in_specs=specs + [pl.BlockSpec(memory_space=pltpu.VMEM)] * len(held),
            scratch_shapes=scratch,
        )(*operands[: len(specs)], *held)

    return call


def block_step(expression, current, next_packed, covariates):
    rows, genes = expression.shape
    variants = current.shape[1]
    covs = covariates.shape[1]
    held, words = next_packed.shape
    share = words // RING
    total = rows * RING * LOCAL
    own_genes = genes // (RING * LOCAL)
    q = lax.axis_index("q")
    j = lax.axis_index("j")

    count = RING * held
    height = count + 8 + covs // 2
    local_genes = genes // LOCAL
    at = local_genes + variants
    moved, packed = kernel(
        prepare_kernel,
        (
            jax.ShapeDtypeStruct((LOCAL * rows, at + 2 * covs), BF16),
            pltpu.VMEM((RING * 8, 128), jnp.int32),
        ),
        [pltpu.VMEM] * 4,
    )(expression, current, covariates, next_packed)
    moved = exchange(moved, "j")
    packed = packed.reshape(RING, 8, 128)
    pieces = []
    for ahead in range(RING):
        piece = lax.dynamic_index_in_dim(packed, (q + ahead) % RING, 0, keepdims=False)
        pieces.append(shift(piece, ahead) if ahead else piece)

    where = jnp.stack([j, q]).astype(jnp.int32)
    half = own_genes // 2
    blocks = kernel(
        functools.partial(product_kernel, local_genes, variants),
        [pltpu.VMEM((half, variants), F32)] * (2 * RING),
        [pltpu.SMEM],
        [pltpu.VMEM((local_genes, variants), F32)],
    )(where, moved)

    stats = kernel(
        functools.partial(stats_kernel, held, share, at, covs),
        jax.ShapeDtypeStruct((height, 2 * covs), F32),
        [pltpu.SMEM],
    )(where, moved, *pieces)
    sums = [stats]
    ahead, behind = stats, stats
    for hop in range(1, RING // 2 + 1):
        ahead = shift(ahead, 1)
        sums.append(ahead)
        if hop < RING // 2:
            behind = shift(behind, -1)
            sums.append(behind)
    placed = kernel(
        functools.partial(finish_kernel, held, share, at, variants, covs, float(total)),
        jax.ShapeDtypeStruct((LOCAL * rows, variants), BF16),
        [pltpu.SMEM],
    )(where, moved, *pieces, *sums)
    placed = exchange(placed, "j")
    next_block = jnp.sum(placed.reshape(LOCAL, rows, variants).astype(F32), axis=0).astype(BF16)

    scale_factor = float(total) ** (-0.5)
    far = RING // 2
    carried = {}
    for step in range(1, far + 1):
        for name, way, part, late in STREAMS:
            if step + late <= far:
                block = blocks[2 * (way * (far + 1 - step - late) % RING) + part]
                held_sum = carried[name] + block if name in carried else block
                carried[name] = shift(held_sum, way)
    scores = kernel(
        functools.partial(total_kernel, scale_factor),
        jax.ShapeDtypeStruct((own_genes, variants), F32),
    )(*blocks[:2], *(carried[name] for name in ("right_a", "right_b", "left_a", "left_b")))
    return (scores, next_block)


STREAMS = (("right_a", 1, 0, 0), ("left_b", -1, 1, 0), ("right_b", 1, 1, 1), ("left_a", -1, 0, 1))


def solution(mesh):
    split = Mesh(mesh.devices.reshape(mesh.shape["parts"], RING, LOCAL), ("parts", "q", "j"))
    return jax.shard_map(
        block_step, mesh=split, in_specs=(SPEC,) * 4, out_specs=(SPEC,) * 2, check_vma=False
    )
```

profile of v0, /device:TPU:33, one launch (start us, length us, event | category | flops | bytes accessed | tf_op | source)
XLA Modules:
  0.0 129.7 jit_solution(10115249640100612364)
XLA Ops:
  0.6 3.0 %shard_map.59 = (bf16[512,1664]{1,0:T(8,128)(2,1)}, s32[64,128]{1,0:T(8,128)S(1)}) custom-call(bf16[32,20480]{1,0:T(8,128)(2,1)} %expression_ref.1, bf16[32,256]{1,0:T(8,128)(2,1)} %current_ref.1, f32[32,64]{1,0:T(8,128)} %covariates_ref.1, s32[2,256]{1,0:T(2,128)} %packed_ref.1), custom_call_target="tpu_custom_call" | custom-call | tf_op jit(solution)/shard_map/pallas_call | solution.py:163
  3.7 23.9 %all-to-all-start = ((bf16[16,32,1664]{2,1,0:T(8,128)(2,1)}), bf16[16,32,1664]{2,1,0:T(8,128)(2,1)S(1)}, u32[]{:S(2)}, u32[]{:S(2)}) async-start(bf16[16,32,1664]{2,1,0:T(8,128)(2,1)} %bitcast.26), calls=%async_computation | async-start | bytes 3407872 | tf_op jit(solution)/shard_map/all_to_all | solution.py:150
  27.6 5.2 %collective-permute-start.20 = (s32[8,128]{1,0:T(8,128)S(1)}, s32[8,128]{1,0:T(8,128)S(1)}, u32[]{:S(2)}, u32[]{:S(2)}) collective-permute-start(s32[8,128]{1,0:T(8,128)S(1)} %get-tuple-element.38), channel_id=1, source_target_pairs={{0,112},{16,0},{32,16},{48,32},{64,48},{80,64},{96,80},{112,96},{1... | collective-permute-start | bytes 12296 | tf_op jit(solution)/shard_map/ppermute | solution.py:154
  32.8 10.3 %collective-permute-start.17 = (s32[8,128]{1,0:T(8,128)S(1)}, s32[8,128]{1,0:T(8,128)S(1)}, u32[]{:S(2)}, u32[]{:S(2)}) collective-permute-start(s32[8,128]{1,0:T(8,128)S(1)} %get-tuple-element.41), channel_id=1, source_target_pairs={{0,64},{16,80},{32,96},{48,112},{64,0},{80,16},{96,32},{112,48},{1... | collective-permute-start | bytes 12296 | tf_op jit(solution)/shard_map/ppermute | solution.py:154
  43.1 2.2 %collective-permute-start.15 = (s32[8,128]{1,0:T(8,128)S(1)}, s32[8,128]{1,0:T(8,128)S(1)}, u32[]{:S(2)}, u32[]{:S(2)}) collective-permute-start(s32[8,128]{1,0:T(8,128)S(1)} %get-tuple-element.43), channel_id=1, source_target_pairs={{0,32},{16,48},{32,64},{48,80},{64,96},{80,112},{96,0},{112,16},{1... | collective-permute-start | bytes 12296 | tf_op jit(solution)/shard_map/ppermute | solution.py:154
  45.4 3.3 %collective-permute-start.14 = (s32[8,128]{1,0:T(8,128)S(1)}, s32[8,128]{1,0:T(8,128)S(1)}, u32[]{:S(2)}, u32[]{:S(2)}) collective-permute-start(s32[8,128]{1,0:T(8,128)S(1)} %get-tuple-element.44), channel_id=1, source_target_pairs={{0,16},{16,32},{32,48},{48,64},{64,80},{80,96},{96,112},{112,0},{1... | collective-permute-start | bytes 12296 | tf_op jit(solution)/shard_map/ppermute | solution.py:154
  49.3 1.7 %collective-permute-done.17.refs_4_ = s32[8,128]{1,0:T(8,128)S(1)} collective-permute-done((s32[8,128]{1,0:T(8,128)S(1)}, s32[8,128]{1,0:T(8,128)S(1)}, u32[]{:S(2)}, u32[]{:S(2)}) %collective-permute-start.17) | collective-permute-done | bytes 4128 | tf_op jit(solution)/shard_map/ppermute | solution.py:154
  51.0 1.5 %collective-permute-done.16.refs_3_ = s32[8,128]{1,0:T(8,128)S(1)} collective-permute-done((s32[8,128]{1,0:T(8,128)S(1)}, s32[8,128]{1,0:T(8,128)S(1)}, u32[]{:S(2)}, u32[]{:S(2)}) %collective-permute-start.16) | collective-permute-done | bytes 4128 | tf_op jit(solution)/shard_map/ppermute | solution.py:154
  53.3 2.0 %shard_map.62.refs_8_ = f32[56,128]{1,0:T(8,128)} custom-call(s32[2]{0:T(128)} %pad_add_fusion.where_ref, bf16[512,1664]{1,0:T(8,128)(2,1)S(1)} %bitcast.22, s32[8,128]{1,0:T(8,128)S(1)} %get-tuple-element.45.refs_0_, s32[8,128]{1,0:T(8,128)S(1)} %collective-permute-done.14.refs_1_, s32[8,128]{1,0:T(8,128)S(1)} %collective-permute-done.15.refs_2_, ...), custom_call_target="tpu_custom_call" | custom-call | tf_op jit(solution)/shard_map/pallas_call | solution.py:163
  56.4 2.0 %collective-permute-start.21 = (f32[56,128]{1,0:T(8,128)}, f32[56,128]{1,0:T(8,128)S(1)}, u32[]{:S(2)}, u32[]{:S(2)}) collective-permute-start(f32[56,128]{1,0:T(8,128)} %shard_map.62.refs_8_), channel_id=1, source_target_pairs={{0,16},{16,32},{32,48},{48,64},{64,80},{80,96},{96,112},{112,0},{1... | collective-permute-start | bytes 86024 | tf_op jit(solution)/shard_map/ppermute | solution.py:154
  58.4 1.6 %collective-permute-start.22 = (f32[56,128]{1,0:T(8,128)}, f32[56,128]{1,0:T(8,128)S(1)}, u32[]{:S(2)}, u32[]{:S(2)}) collective-permute-start(f32[56,128]{1,0:T(8,128)} %shard_map.62.refs_8_), channel_id=1, source_target_pairs={{0,112},{16,0},{32,16},{48,32},{64,48},{80,64},{96,80},{112,96},{1... | collective-permute-start | bytes 86024 | tf_op jit(solution)/shard_map/ppermute | solution.py:154
  60.0 1.5 %collective-permute-done.21.refs_9_ = f32[56,128]{1,0:T(8,128)S(1)} collective-permute-done((f32[56,128]{1,0:T(8,128)}, f32[56,128]{1,0:T(8,128)S(1)}, u32[]{:S(2)}, u32[]{:S(2)}) %collective-permute-start.21) | collective-permute-done | bytes 28704 | tf_op jit(solution)/shard_map/ppermute | solution.py:154
  62.8 2.2 %collective-permute-start.24 = (f32[56,128]{1,0:T(8,128)S(1)}, f32[56,128]{1,0:T(8,128)S(1)}, u32[]{:S(2)}, u32[]{:S(2)}) collective-permute-start(f32[56,128]{1,0:T(8,128)S(1)} %collective-permute-done.22.refs_10_), channel_id=1, source_target_pairs={{0,112},{16,0},{32,16},{48,32},{64,48},{80,64},{96,80},{112,96},{1... | collective-permute-start | bytes 86024 | tf_op jit(solution)/shard_map/ppermute | solution.py:154
  65.0 1.5 %collective-permute-done.23.refs_11_ = f32[56,128]{1,0:T(8,128)S(1)} collective-permute-done((f32[56,128]{1,0:T(8,128)S(1)}, f32[56,128]{1,0:T(8,128)S(1)}, u32[]{:S(2)}, u32[]{:S(2)}) %collective-permute-start.23) | collective-permute-done | bytes 28704 | tf_op jit(solution)/shard_map/ppermute | solution.py:154
  68.0 2.2 %collective-permute-start.26 = (f32[56,128]{1,0:T(8,128)S(1)}, f32[56,128]{1,0:T(8,128)S(1)}, u32[]{:S(2)}, u32[]{:S(2)}) collective-permute-start(f32[56,128]{1,0:T(8,128)S(1)} %collective-permute-done.24.refs_12_), channel_id=1, source_target_pairs={{0,112},{16,0},{32,16},{48,32},{64,48},{80,64},{96,80},{112,96},{1... | collective-permute-start | bytes 86024 | tf_op jit(solution)/shard_map/ppermute | solution.py:154
  70.2 1.6 %collective-permute-done.25.refs_13_ = f32[56,128]{1,0:T(8,128)S(1)} collective-permute-done((f32[56,128]{1,0:T(8,128)S(1)}, f32[56,128]{1,0:T(8,128)S(1)}, u32[]{:S(2)}, u32[]{:S(2)}) %collective-permute-start.25) | collective-permute-done | bytes 28704 | tf_op jit(solution)/shard_map/ppermute | solution.py:154
  73.0 3.7 %collective-permute-done.27.refs_15_ = f32[56,128]{1,0:T(8,128)S(1)} collective-permute-done((f32[56,128]{1,0:T(8,128)S(1)}, f32[56,128]{1,0:T(8,128)S(1)}, u32[]{:S(2)}, u32[]{:S(2)}) %collective-permute-start.27) | collective-permute-done | bytes 28704 | tf_op jit(solution)/shard_map/ppermute | solution.py:154
  76.6 1.5 %copy-done.1 = bf16[16,32,1664]{2,1,0:T(8,128)(2,1)S(1)} copy-done((bf16[16,32,1664]{2,1,0:T(8,128)(2,1)S(1)}, bf16[16,32,1664]{2,1,0:T(8,128)(2,1)}, u32[]{:S(2)}) %copy-start.1) | copy-done | bytes 1703960
  78.8 2.2 %shard_map.63 = bf16[512,256]{1,0:T(8,128)(2,1)} custom-call(s32[2]{0:T(128)} %pad_add_fusion.where_ref, bf16[512,1664]{1,0:T(8,128)(2,1)S(1)} %bitcast.23, s32[8,128]{1,0:T(8,128)S(1)} %get-tuple-element.45.refs_0_, s32[8,128]{1,0:T(8,128)S(1)} %collective-permute-done.14.refs_1_, s32[8,128]{1,0:T(8,128)S(1)} %collective-permute-done.15.refs_2_, ...), custom_call_target="tpu_custom_call" | custom-call | tf_op jit(solution)/shard_map/pallas_call | solution.py:163
  81.0 15.0 %all-to-all-start.1 = ((bf16[16,32,256]{2,1,0:T(8,128)(2,1)}), bf16[16,32,256]{2,1,0:T(8,128)(2,1)S(1)}, u32[]{:S(2)}, u32[]{:S(2)}) async-start(bf16[16,32,256]{2,1,0:T(8,128)(2,1)} %bitcast.27), calls=%async_computation.1 | async-start | bytes 524288 | tf_op jit(solution)/shard_map/all_to_all | solution.py:150
  96.0 1.3 shard_map.60
  97.5 3.5 %collective-permute-start.10 = (f32[80,256]{1,0:T(8,128)S(1)}, f32[80,256]{1,0:T(8,128)S(1)}, u32[]{:S(2)}, u32[]{:S(2)}) collective-permute-start(f32[80,256]{1,0:T(8,128)S(1)} %get-tuple-element.33), channel_id=1, source_target_pairs={{0,112},{16,0},{32,16},{48,32},{64,48},{80,64},{96,80},{112,96},{1... | collective-permute-start | bytes 245768 | tf_op jit(solution)/shard_map/ppermute | solution.py:154
  101.1 3.5 %collective-permute-start.7 = (f32[80,256]{1,0:T(8,128)S(1)}, f32[80,256]{1,0:T(8,128)S(1)}, u32[]{:S(2)}, u32[]{:S(2)}) collective-permute-start(f32[80,256]{1,0:T(8,128)S(1)} %get-tuple-element.30), channel_id=1, source_target_pairs={{0,112},{16,0},{32,16},{48,32},{64,48},{80,64},{96,80},{112,96},{1... | collective-permute-start | bytes 245768 | tf_op jit(solution)/shard_map/ppermute | solution.py:154
  104.8 3.6 %collective-permute-start.11 = (f32[80,256]{1,0:T(8,128)S(1)}, f32[80,256]{1,0:T(8,128)S(1)}, u32[]{:S(2)}, u32[]{:S(2)}) collective-permute-start(f32[80,256]{1,0:T(8,128)S(1)} %add.108), channel_id=1, source_target_pairs={{0,112},{16,0},{32,16},{48,32},{64,48},{80,64},{96,80},{112,96},{1... | collective-permute-start | bytes 245768 | tf_op jit(solution)/shard_map/ppermute | solution.py:154
  108.7 3.6 %collective-permute-start.8 = (f32[80,256]{1,0:T(8,128)S(1)}, f32[80,256]{1,0:T(8,128)S(1)}, u32[]{:S(2)}, u32[]{:S(2)}) collective-permute-start(f32[80,256]{1,0:T(8,128)S(1)} %add.106), channel_id=1, source_target_pairs={{0,112},{16,0},{32,16},{48,32},{64,48},{80,64},{96,80},{112,96},{1... | collective-permute-start | bytes 245768 | tf_op jit(solution)/shard_map/ppermute | solution.py:154
  113.2 2.8 %collective-permute-start.12 = (f32[80,256]{1,0:T(8,128)S(1)}, f32[80,256]{1,0:T(8,128)S(1)}, u32[]{:S(2)}, u32[]{:S(2)}) collective-permute-start(f32[80,256]{1,0:T(8,128)S(1)} %add.109), channel_id=1, source_target_pairs={{0,112},{16,0},{32,16},{48,32},{64,48},{80,64},{96,80},{112,96},{1... | collective-permute-start | bytes 245768 | tf_op jit(solution)/shard_map/ppermute | solution.py:154
  116.1 1.5 %collective-permute-start.6 = (f32[80,256]{1,0:T(8,128)S(1)}, f32[80,256]{1,0:T(8,128)S(1)}, u32[]{:S(2)}, u32[]{:S(2)}) collective-permute-start(f32[80,256]{1,0:T(8,128)S(1)} %add.105), channel_id=1, source_target_pairs={{0,16},{16,32},{32,48},{48,64},{64,80},{80,96},{96,112},{112,0},{1... | collective-permute-start | bytes 245768 | tf_op jit(solution)/shard_map/ppermute | solution.py:154
  117.7 2.3 %collective-permute-start.9 = (f32[80,256]{1,0:T(8,128)S(1)}, f32[80,256]{1,0:T(8,128)S(1)}, u32[]{:S(2)}, u32[]{:S(2)}) collective-permute-start(f32[80,256]{1,0:T(8,128)S(1)} %add.107), channel_id=1, source_target_pairs={{0,112},{16,0},{32,16},{48,32},{64,48},{80,64},{96,80},{112,96},{1... | collective-permute-start | bytes 245768 | tf_op jit(solution)/shard_map/ppermute | solution.py:154
  120.0 2.0 %collective-permute-start.3 = (f32[80,256]{1,0:T(8,128)S(1)}, f32[80,256]{1,0:T(8,128)S(1)}, u32[]{:S(2)}, u32[]{:S(2)}) collective-permute-start(f32[80,256]{1,0:T(8,128)S(1)} %add.103), channel_id=1, source_target_pairs={{0,16},{16,32},{32,48},{48,64},{64,80},{80,96},{96,112},{112,0},{1... | collective-permute-start | bytes 245768 | tf_op jit(solution)/shard_map/ppermute | solution.py:154
  121.9 1.8 %collective-permute-start.13 = (f32[80,256]{1,0:T(8,128)S(1)}, f32[80,256]{1,0:T(8,128)S(1)}, u32[]{:S(2)}, u32[]{:S(2)}) collective-permute-start(f32[80,256]{1,0:T(8,128)S(1)} %add.110), channel_id=1, source_target_pairs={{0,112},{16,0},{32,16},{48,32},{64,48},{80,64},{96,80},{112,96},{1... | collective-permute-start | bytes 245768 | tf_op jit(solution)/shard_map/ppermute | solution.py:154
  123.8 2.9 %collective-permute-done.3.refs_2_ = f32[80,256]{1,0:T(8,128)S(1)} collective-permute-done((f32[80,256]{1,0:T(8,128)S(1)}, f32[80,256]{1,0:T(8,128)S(1)}, u32[]{:S(2)}, u32[]{:S(2)}) %collective-permute-start.3) | collective-permute-done | bytes 81952 | tf_op jit(solution)/shard_map/ppermute | solution.py:154
  126.7 1.7 %collective-permute-done.13.refs_5_ = f32[80,256]{1,0:T(8,128)S(1)} collective-permute-done((f32[80,256]{1,0:T(8,128)S(1)}, f32[80,256]{1,0:T(8,128)S(1)}, u32[]{:S(2)}, u32[]{:S(2)}) %collective-permute-start.13) | collective-permute-done | bytes 81952 | tf_op jit(solution)/shard_map/ppermute | solution.py:154
  (52 shorter events, 10.5 us)
Async XLA Ops:
  3.7 49.6 %all-to-all-start = ((bf16[16,32,1664]{2,1,0:T(8,128)(2,1)}), bf16[16,32,1664]{2,1,0:T(8,128)(2,1)S(1)}, u32[]{:S(2)}, u32[]{:S(2)}) async-start(bf16[16,32,1664]{2,1,0:T(8,128)(2,1)} %bitcast.26), calls=%async_computation | async-start | bytes 3407872 | tf_op jit(solution)/shard_map/all_to_all | solution.py:150
  27.6 15.5 %collective-permute-start.20 = (s32[8,128]{1,0:T(8,128)S(1)}, s32[8,128]{1,0:T(8,128)S(1)}, u32[]{:S(2)}, u32[]{:S(2)}) collective-permute-start(s32[8,128]{1,0:T(8,128)S(1)} %get-tuple-element.38), channel_id=1, source_target_pairs={{0,112},{16,0},{32,16},{48,32},{64,48},{80,64},{96,80},{112,96},{1... | collective-permute-start | bytes 12296 | tf_op jit(solution)/shard_map/ppermute | solution.py:154
  32.8 12.6 %collective-permute-start.19 = (s32[8,128]{1,0:T(8,128)S(1)}, s32[8,128]{1,0:T(8,128)S(1)}, u32[]{:S(2)}, u32[]{:S(2)}) collective-permute-start(s32[8,128]{1,0:T(8,128)S(1)} %get-tuple-element.39), channel_id=1, source_target_pairs={{0,96},{16,112},{32,0},{48,16},{64,32},{80,48},{96,64},{112,80},{1... | collective-permute-start | bytes 12296 | tf_op jit(solution)/shard_map/ppermute | solution.py:154
  32.8 16.5 %collective-permute-start.18 = (s32[8,128]{1,0:T(8,128)S(1)}, s32[8,128]{1,0:T(8,128)S(1)}, u32[]{:S(2)}, u32[]{:S(2)}) collective-permute-start(s32[8,128]{1,0:T(8,128)S(1)} %get-tuple-element.40), channel_id=1, source_target_pairs={{0,80},{16,96},{32,112},{48,0},{64,16},{80,32},{96,48},{112,64},{1... | collective-permute-start | bytes 12296 | tf_op jit(solution)/shard_map/ppermute | solution.py:154
  32.8 18.2 %collective-permute-start.17 = (s32[8,128]{1,0:T(8,128)S(1)}, s32[8,128]{1,0:T(8,128)S(1)}, u32[]{:S(2)}, u32[]{:S(2)}) collective-permute-start(s32[8,128]{1,0:T(8,128)S(1)} %get-tuple-element.41), channel_id=1, source_target_pairs={{0,64},{16,80},{32,96},{48,112},{64,0},{80,16},{96,32},{112,48},{1... | collective-permute-start | bytes 12296 | tf_op jit(solution)/shard_map/ppermute | solution.py:154
  43.1 9.4 %collective-permute-start.16 = (s32[8,128]{1,0:T(8,128)S(1)}, s32[8,128]{1,0:T(8,128)S(1)}, u32[]{:S(2)}, u32[]{:S(2)}) collective-permute-start(s32[8,128]{1,0:T(8,128)S(1)} %get-tuple-element.42), channel_id=1, source_target_pairs={{0,48},{16,64},{32,80},{48,96},{64,112},{80,0},{96,16},{112,32},{1... | collective-permute-start | bytes 12296 | tf_op jit(solution)/shard_map/ppermute | solution.py:154
  43.1 9.4 %collective-permute-start.15 = (s32[8,128]{1,0:T(8,128)S(1)}, s32[8,128]{1,0:T(8,128)S(1)}, u32[]{:S(2)}, u32[]{:S(2)}) collective-permute-start(s32[8,128]{1,0:T(8,128)S(1)} %get-tuple-element.43), channel_id=1, source_target_pairs={{0,32},{16,48},{32,64},{48,80},{64,96},{80,112},{96,0},{112,16},{1... | collective-permute-start | bytes 12296 | tf_op jit(solution)/shard_map/ppermute | solution.py:154
  45.4 7.9 %collective-permute-start.14 = (s32[8,128]{1,0:T(8,128)S(1)}, s32[8,128]{1,0:T(8,128)S(1)}, u32[]{:S(2)}, u32[]{:S(2)}) collective-permute-start(s32[8,128]{1,0:T(8,128)S(1)} %get-tuple-element.44), channel_id=1, source_target_pairs={{0,16},{16,32},{32,48},{48,64},{64,80},{80,96},{96,112},{112,0},{1... | collective-permute-start | bytes 12296 | tf_op jit(solution)/shard_map/ppermute | solution.py:154
  55.2 1.2 copy-start
  56.4 5.0 %collective-permute-start.21 = (f32[56,128]{1,0:T(8,128)}, f32[56,128]{1,0:T(8,128)S(1)}, u32[]{:S(2)}, u32[]{:S(2)}) collective-permute-start(f32[56,128]{1,0:T(8,128)} %shard_map.62.refs_8_), channel_id=1, source_target_pairs={{0,16},{16,32},{32,48},{48,64},{64,80},{80,96},{96,112},{112,0},{1... | collective-permute-start | bytes 86024 | tf_op jit(solution)/shard_map/ppermute | solution.py:154
  58.4 4.4 %collective-permute-start.22 = (f32[56,128]{1,0:T(8,128)}, f32[56,128]{1,0:T(8,128)S(1)}, u32[]{:S(2)}, u32[]{:S(2)}) collective-permute-start(f32[56,128]{1,0:T(8,128)} %shard_map.62.refs_8_), channel_id=1, source_target_pairs={{0,112},{16,0},{32,16},{48,32},{64,48},{80,64},{96,80},{112,96},{1... | collective-permute-start | bytes 86024 | tf_op jit(solution)/shard_map/ppermute | solution.py:154
  61.5 5.1 %collective-permute-start.23 = (f32[56,128]{1,0:T(8,128)S(1)}, f32[56,128]{1,0:T(8,128)S(1)}, u32[]{:S(2)}, u32[]{:S(2)}) collective-permute-start(f32[56,128]{1,0:T(8,128)S(1)} %collective-permute-done.21.refs_9_), channel_id=1, source_target_pairs={{0,16},{16,32},{32,48},{48,64},{64,80},{80,96},{96,112},{112,0},{1... | collective-permute-start | bytes 86024 | tf_op jit(solution)/shard_map/ppermute | solution.py:154
  62.8 5.1 %collective-permute-start.24 = (f32[56,128]{1,0:T(8,128)S(1)}, f32[56,128]{1,0:T(8,128)S(1)}, u32[]{:S(2)}, u32[]{:S(2)}) collective-permute-start(f32[56,128]{1,0:T(8,128)S(1)} %collective-permute-done.22.refs_10_), channel_id=1, source_target_pairs={{0,112},{16,0},{32,16},{48,32},{64,48},{80,64},{96,80},{112,96},{1... | collective-permute-start | bytes 86024 | tf_op jit(solution)/shard_map/ppermute | solution.py:154
  66.6 5.1 %collective-permute-start.25 = (f32[56,128]{1,0:T(8,128)S(1)}, f32[56,128]{1,0:T(8,128)S(1)}, u32[]{:S(2)}, u32[]{:S(2)}) collective-permute-start(f32[56,128]{1,0:T(8,128)S(1)} %collective-permute-done.23.refs_11_), channel_id=1, source_target_pairs={{0,16},{16,32},{32,48},{48,64},{64,80},{80,96},{96,112},{112,0},{1... | collective-permute-start | bytes 86024 | tf_op jit(solution)/shard_map/ppermute | solution.py:154
  68.0 5.0 %collective-permute-start.26 = (f32[56,128]{1,0:T(8,128)S(1)}, f32[56,128]{1,0:T(8,128)S(1)}, u32[]{:S(2)}, u32[]{:S(2)}) collective-permute-start(f32[56,128]{1,0:T(8,128)S(1)} %collective-permute-done.24.refs_12_), channel_id=1, source_target_pairs={{0,112},{16,0},{32,16},{48,32},{64,48},{80,64},{96,80},{112,96},{1... | collective-permute-start | bytes 86024 | tf_op jit(solution)/shard_map/ppermute | solution.py:154
  71.7 4.9 %collective-permute-start.27 = (f32[56,128]{1,0:T(8,128)S(1)}, f32[56,128]{1,0:T(8,128)S(1)}, u32[]{:S(2)}, u32[]{:S(2)}) collective-permute-start(f32[56,128]{1,0:T(8,128)S(1)} %collective-permute-done.25.refs_13_), channel_id=1, source_target_pairs={{0,16},{16,32},{32,48},{48,64},{64,80},{80,96},{96,112},{112,0},{1... | collective-permute-start | bytes 86024 | tf_op jit(solution)/shard_map/ppermute | solution.py:154
  76.6 1.5 %copy-start.1 = (bf16[16,32,1664]{2,1,0:T(8,128)(2,1)S(1)}, bf16[16,32,1664]{2,1,0:T(8,128)(2,1)}, u32[]{:S(2)}) copy-start(bf16[16,32,1664]{2,1,0:T(8,128)(2,1)} %copy-done) | copy-start | bytes 5111812
  81.0 48.1 %all-to-all-start.1 = ((bf16[16,32,256]{2,1,0:T(8,128)(2,1)}), bf16[16,32,256]{2,1,0:T(8,128)(2,1)S(1)}, u32[]{:S(2)}, u32[]{:S(2)}) async-start(bf16[16,32,256]{2,1,0:T(8,128)(2,1)} %bitcast.27), calls=%async_computation.1 | async-start | bytes 524288 | tf_op jit(solution)/shard_map/all_to_all | solution.py:150
  97.3 7.3 %collective-permute-start = (f32[80,256]{1,0:T(8,128)S(1)}, f32[80,256]{1,0:T(8,128)S(1)}, u32[]{:S(2)}, u32[]{:S(2)}) collective-permute-start(f32[80,256]{1,0:T(8,128)S(1)} %get-tuple-element.23), channel_id=1, source_target_pairs={{0,16},{16,32},{32,48},{48,64},{64,80},{80,96},{96,112},{112,0},{1... | collective-permute-start | bytes 245768 | tf_op jit(solution)/shard_map/ppermute | solution.py:154
  97.5 7.3 %collective-permute-start.10 = (f32[80,256]{1,0:T(8,128)S(1)}, f32[80,256]{1,0:T(8,128)S(1)}, u32[]{:S(2)}, u32[]{:S(2)}) collective-permute-start(f32[80,256]{1,0:T(8,128)S(1)} %get-tuple-element.33), channel_id=1, source_target_pairs={{0,112},{16,0},{32,16},{48,32},{64,48},{80,64},{96,80},{112,96},{1... | collective-permute-start | bytes 245768 | tf_op jit(solution)/shard_map/ppermute | solution.py:154
  101.0 7.4 %collective-permute-start.4 = (f32[80,256]{1,0:T(8,128)S(1)}, f32[80,256]{1,0:T(8,128)S(1)}, u32[]{:S(2)}, u32[]{:S(2)}) collective-permute-start(f32[80,256]{1,0:T(8,128)S(1)} %get-tuple-element.27), channel_id=1, source_target_pairs={{0,16},{16,32},{32,48},{48,64},{64,80},{80,96},{96,112},{112,0},{1... | collective-permute-start | bytes 245768 | tf_op jit(solution)/shard_map/ppermute | solution.py:154
  101.1 7.6 %collective-permute-start.7 = (f32[80,256]{1,0:T(8,128)S(1)}, f32[80,256]{1,0:T(8,128)S(1)}, u32[]{:S(2)}, u32[]{:S(2)}) collective-permute-start(f32[80,256]{1,0:T(8,128)S(1)} %get-tuple-element.30), channel_id=1, source_target_pairs={{0,112},{16,0},{32,16},{48,32},{64,48},{80,64},{96,80},{112,96},{1... | collective-permute-start | bytes 245768 | tf_op jit(solution)/shard_map/ppermute | solution.py:154
  104.6 7.7 %collective-permute-start.1 = (f32[80,256]{1,0:T(8,128)S(1)}, f32[80,256]{1,0:T(8,128)S(1)}, u32[]{:S(2)}, u32[]{:S(2)}) collective-permute-start(f32[80,256]{1,0:T(8,128)S(1)} %add.101), channel_id=1, source_target_pairs={{0,16},{16,32},{32,48},{48,64},{64,80},{80,96},{96,112},{112,0},{1... | collective-permute-start | bytes 245768 | tf_op jit(solution)/shard_map/ppermute | solution.py:154
  104.8 8.4 %collective-permute-start.11 = (f32[80,256]{1,0:T(8,128)S(1)}, f32[80,256]{1,0:T(8,128)S(1)}, u32[]{:S(2)}, u32[]{:S(2)}) collective-permute-start(f32[80,256]{1,0:T(8,128)S(1)} %add.108), channel_id=1, source_target_pairs={{0,112},{16,0},{32,16},{48,32},{64,48},{80,64},{96,80},{112,96},{1... | collective-permute-start | bytes 245768 | tf_op jit(solution)/shard_map/ppermute | solution.py:154
  108.4 7.7 %collective-permute-start.5 = (f32[80,256]{1,0:T(8,128)S(1)}, f32[80,256]{1,0:T(8,128)S(1)}, u32[]{:S(2)}, u32[]{:S(2)}) collective-permute-start(f32[80,256]{1,0:T(8,128)S(1)} %add.104), channel_id=1, source_target_pairs={{0,16},{16,32},{32,48},{48,64},{64,80},{80,96},{96,112},{112,0},{1... | collective-permute-start | bytes 245768 | tf_op jit(solution)/shard_map/ppermute | solution.py:154
  108.7 9.0 %collective-permute-start.8 = (f32[80,256]{1,0:T(8,128)S(1)}, f32[80,256]{1,0:T(8,128)S(1)}, u32[]{:S(2)}, u32[]{:S(2)}) collective-permute-start(f32[80,256]{1,0:T(8,128)S(1)} %add.106), channel_id=1, source_target_pairs={{0,112},{16,0},{32,16},{48,32},{64,48},{80,64},{96,80},{112,96},{1... | collective-permute-start | bytes 245768 | tf_op jit(solution)/shard_map/ppermute | solution.py:154
  112.3 7.7 %collective-permute-start.2 = (f32[80,256]{1,0:T(8,128)S(1)}, f32[80,256]{1,0:T(8,128)S(1)}, u32[]{:S(2)}, u32[]{:S(2)}) collective-permute-start(f32[80,256]{1,0:T(8,128)S(1)} %add.102), channel_id=1, source_target_pairs={{0,16},{16,32},{32,48},{48,64},{64,80},{80,96},{96,112},{112,0},{1... | collective-permute-start | bytes 245768 | tf_op jit(solution)/shard_map/ppermute | solution.py:154
  113.2 8.7 %collective-permute-start.12 = (f32[80,256]{1,0:T(8,128)S(1)}, f32[80,256]{1,0:T(8,128)S(1)}, u32[]{:S(2)}, u32[]{:S(2)}) collective-permute-start(f32[80,256]{1,0:T(8,128)S(1)} %add.109), channel_id=1, source_target_pairs={{0,112},{16,0},{32,16},{48,32},{64,48},{80,64},{96,80},{112,96},{1... | collective-permute-start | bytes 245768 | tf_op jit(solution)/shard_map/ppermute | solution.py:154
  116.1 7.7 %collective-permute-start.6 = (f32[80,256]{1,0:T(8,128)S(1)}, f32[80,256]{1,0:T(8,128)S(1)}, u32[]{:S(2)}, u32[]{:S(2)}) collective-permute-start(f32[80,256]{1,0:T(8,128)S(1)} %add.105), channel_id=1, source_target_pairs={{0,16},{16,32},{32,48},{48,64},{64,80},{80,96},{96,112},{112,0},{1... | collective-permute-start | bytes 245768 | tf_op jit(solution)/shard_map/ppermute | solution.py:154
  117.7 6.1 %collective-permute-start.9 = (f32[80,256]{1,0:T(8,128)S(1)}, f32[80,256]{1,0:T(8,128)S(1)}, u32[]{:S(2)}, u32[]{:S(2)}) collective-permute-start(f32[80,256]{1,0:T(8,128)S(1)} %add.107), channel_id=1, source_target_pairs={{0,112},{16,0},{32,16},{48,32},{64,48},{80,64},{96,80},{112,96},{1... | collective-permute-start | bytes 245768 | tf_op jit(solution)/shard_map/ppermute | solution.py:154
  120.0 6.7 %collective-permute-start.3 = (f32[80,256]{1,0:T(8,128)S(1)}, f32[80,256]{1,0:T(8,128)S(1)}, u32[]{:S(2)}, u32[]{:S(2)}) collective-permute-start(f32[80,256]{1,0:T(8,128)S(1)} %add.103), channel_id=1, source_target_pairs={{0,16},{16,32},{32,48},{48,64},{64,80},{80,96},{96,112},{112,0},{1... | collective-permute-start | bytes 245768 | tf_op jit(solution)/shard_map/ppermute | solution.py:154
  121.9 6.4 %collective-permute-start.13 = (f32[80,256]{1,0:T(8,128)S(1)}, f32[80,256]{1,0:T(8,128)S(1)}, u32[]{:S(2)}, u32[]{:S(2)}) collective-permute-start(f32[80,256]{1,0:T(8,128)S(1)} %add.110), channel_id=1, source_target_pairs={{0,112},{16,0},{32,16},{48,32},{64,48},{80,64},{96,80},{112,96},{1... | collective-permute-start | bytes 245768 | tf_op jit(solution)/shard_map/ppermute | solution.py:154
  (1 other events, 0.7 us)
where the time goes:
time: 131 us; the launch traced here: 130 us
  starting transfers between devices  97.4 us (74%)
  waiting for transfers between devices  17.7 us (14%)
  Pallas kernels  9.14 us (7%)
  local copies, waits for them, and re-layouts  3.42 us (3%)
  other arithmetic  1.41 us (1%)
    ppermute x28, starting transfers between devices, shift(): return lax.ppermute(array, 'q', [(k, (k + by) % RING) for k in range(RING)])  58.4 us
    all_to_all x2, starting transfers between devices, exchange(): return lax.all_to_all(array, axis, split_axis=0, concat_axis=0, tiled=True)  38.9 us
    ppermute x28, waiting for transfers between devices, shift(): return lax.ppermute(array, 'q', [(k, (k + by) % RING) for k in range(RING)])  17.7 us
    pallas_call x5, Pallas kernels, call(): pl.pallas_call(body, out_shape=out_shape, in_specs=specs + [pl.BlockSpec(...  9.14 us
    unnamed x6, local copies, waits for them, and re-layouts  3.41 us
  transfers between devices with their start and end apart: 30, of which 12 were waited for; matrix products, arithmetic and copies ran while one was open for 1% of the time, Pallas kernels for 2%

commit v1 on v0

--- a/solution.py
+++ b/solution.py
@@ -23,19 +23,23 @@
     )
 
 
-def prepare_kernel(expression_ref, current_ref, covariates_ref, packed_ref, out_ref, words_ref):
+def regroup(expression_ref, out_ref, part, own):
     rows, genes = expression_ref.shape
     share = genes // (RING * LOCAL)
+    half = share // 2
+    for j in range(LOCAL):
+        pieces = []
+        for q in range(RING):
+            first = (q * LOCAL + j) * share + part * half
+            pieces.append(expression_ref[:, first : first + half])
+        out_ref[j * rows : (j + 1) * rows, :] = jnp.concatenate(pieces + own, axis=1)
+
+
+def first_kernel(expression_ref, current_ref, covariates_ref, packed_ref, out_ref, words_ref):
     cov = covariates_ref[...]
     high = cov.astype(BF16)
     low = (cov - high.astype(F32)).astype(BF16)
-    own = [current_ref[...], high, low]
-    for j in range(LOCAL):
-        pieces = []
-        for q in range(RING):
-            at = (q * LOCAL + j) * share
-            pieces.append(expression_ref[:, at : at + share])
-        out_ref[j * rows : (j + 1) * rows, :] = jnp.concatenate(pieces + own, axis=1)
+    regroup(expression_ref, out_ref, 0, [current_ref[...], high, low])
     held, words = packed_ref.shape
     split = words // RING
     words_ref[...] = jnp.zeros_like(words_ref)
@@ -44,15 +48,17 @@
         words_ref[q * 8 : q * 8 + held, 0:split] = packed[:, q * split : (q + 1) * split]
 
 
-def product_kernel(genes, variants, where_ref, rows_ref, *refs):
+def second_kernel(expression_ref, out_ref):
+    regroup(expression_ref, out_ref, 1, [])
+
+
+def product_kernel(genes, variants, at, where_ref, rows_ref, own_ref, *refs):
     outs, whole_ref = refs[:-1], refs[-1]
-    whole_ref[...] = dot(rows_ref[:, :genes], rows_ref[:, genes : genes + variants], ((0,), (0,)))
-    share = genes // RING
-    half = share // 2
+    whole_ref[...] = dot(rows_ref[:, :genes], own_ref[:, at : at + variants], ((0,), (0,)))
+    half = genes // RING
     for ahead in range(RING):
-        at = lax.rem(where_ref[1] + ahead, RING) * share
-        for part in range(2):
-            outs[2 * ahead + part][...] = whole_ref[pl.ds(at + part * half, half), :]
+        at = lax.rem(where_ref[1] + ahead, RING) * half
+        outs[ahead][...] = whole_ref[pl.ds(at, half), :]
 
 
 def total_kernel(scale, *refs):
@@ -183,10 +189,10 @@
 
     count = RING * held
     height = count + 8 + covs // 2
-    local_genes = genes // LOCAL
-    at = local_genes + variants
+    half_genes = genes // LOCAL // 2
+    at = half_genes + variants
     moved, packed = kernel(
-        prepare_kernel,
+        first_kernel,
         (
             jax.ShapeDtypeStruct((LOCAL * rows, at + 2 * covs), BF16),
             pltpu.VMEM((RING * 8, 128), jnp.int32),
@@ -194,6 +200,10 @@
         [pltpu.VMEM] * 4,
     )(expression, current, covariates, next_packed)
     moved = exchange(moved, "j")
+    others = kernel(
+        second_kernel, jax.ShapeDtypeStruct((LOCAL * rows, half_genes), BF16), [pltpu.VMEM]
+    )(expression)
+    others = exchange(others, "j")
     packed = packed.reshape(RING, 8, 128)
     pieces = []
     for ahead in range(RING):
@@ -202,12 +212,16 @@
 
     where = jnp.stack([j, q]).astype(jnp.int32)
     half = own_genes // 2
-    blocks = kernel(
-        functools.partial(product_kernel, local_genes, variants),
-        [pltpu.VMEM((half, variants), F32)] * (2 * RING),
-        [pltpu.SMEM],
-        [pltpu.VMEM((local_genes, variants), F32)],
-    )(where, moved)
+
+    def product(array):
+        return kernel(
+            functools.partial(product_kernel, half_genes, variants, half_genes),
+            [pltpu.VMEM((half, variants), F32)] * RING,
+            [pltpu.SMEM],
+            [pltpu.VMEM((half_genes, variants), F32)],
+        )(where, array, moved)
+
+    blocks = (product(moved), product(others))
 
     stats = kernel(
         functools.partial(stats_kernel, held, share, at, covs),
@@ -236,13 +250,13 @@
     for step in range(1, far + 1):
         for name, way, part, late in STREAMS:
             if step + late <= far:
-                block = blocks[2 * (way * (far + 1 - step - late) % RING) + part]
+                block = blocks[part][way * (far + 1 - step - late) % RING]
                 held_sum = carried[name] + block if name in carried else block
                 carried[name] = shift(held_sum, way)
     scores = kernel(
         functools.partial(total_kernel, scale_factor),
         jax.ShapeDtypeStruct((own_genes, variants), F32),
-    )(*blocks[:2], *(carried[name] for name in ("right_a", "right_b", "left_a", "left_b")))
+    )(blocks[0][0], blocks[1][0], *(carried[name] for name in ("right_a", "right_b", "left_a", "left_b")))
     return (scores, next_block)
 
 

time: 131 us -> 152 us (1.16)
  waiting for transfers between devices: 17.7 us -> 37.4 us
  Pallas kernels: 9.14 us -> 12.4 us
  local copies, waits for them, and re-layouts: 3.42 us -> 0.76 us
    all_to_all x2 -> x3, waiting for transfers between devices: 0.01 us -> 13.4 us  [exchange(): return lax.all_to_all(array, axis, split_axis=0, concat_axis=0, tiled=True)]
    ppermute x28, waiting for transfers between devices: 17.7 us -> 24 us  [shift(): return lax.ppermute(array, 'q', [(k, (k + by) % RING) for k in range(RING)])]
    ppermute x28, starting transfers between devices: 58.4 us -> 54.6 us  [shift(): return lax.ppermute(array, 'q', [(k, (k + by) % RING) for k in range(RING)])]
    pallas_call x5 -> x7, Pallas kernels: 9.14 us -> 12.4 us  [call(): pl.pallas_call(body, out_shape=out_shape, in_specs=specs + [pl.BlockSpec(...]
    all_to_all x2 -> x3, starting transfers between devices: 38.9 us -> 42 us  [exchange(): return lax.all_to_all(array, axis, split_axis=0, concat_axis=0, tiled=True)]
    unnamed x6 -> x2, local copies, waits for them, and re-layouts: 3.41 us -> 0.75 us
  transfers between devices with their start and end apart: 30 -> 31, of which waited for: 12 -> 9; matrix products, arithmetic and copies ran while one was open for 1% -> 1% of each run, Pallas kernels for 2% -> 6%
where the time goes in v1:
time: 152 us; the launch traced here: 149 us
  starting transfers between devices  96.6 us (64%)
  waiting for transfers between devices  37.4 us (25%)
  Pallas kernels  12.4 us (8%)
    ppermute x28, starting transfers between devices, shift(): return lax.ppermute(array, 'q', [(k, (k + by) % RING) for k in range(RING)])  54.6 us
    all_to_all x3, starting transfers between devices, exchange(): return lax.all_to_all(array, axis, split_axis=0, concat_axis=0, tiled=True)  42 us
    ppermute x28, waiting for transfers between devices, shift(): return lax.ppermute(array, 'q', [(k, (k + by) % RING) for k in range(RING)])  24 us
    all_to_all x3, waiting for transfers between devices, exchange(): return lax.all_to_all(array, axis, split_axis=0, concat_axis=0, tiled=True)  13.4 us
    pallas_call x7, Pallas kernels, call(): pl.pallas_call(body, out_shape=out_shape, in_specs=specs + [pl.BlockSpec(...  12.4 us
  transfers between devices with their start and end apart: 31, of which 9 were waited for; matrix products, arithmetic and copies ran while one was open for 1% of the time, Pallas kernels for 6%

profile of v1, /device:TPU:33, one launch (start us, length us, event | category | flops | bytes accessed | tf_op | source)
XLA Modules:
  0.0 149.4 jit_solution(16175217381712286884)
XLA Ops:
  0.6 2.8 %shard_map.59 = (bf16[512,1024]{1,0:T(8,128)(2,1)}, s32[64,128]{1,0:T(8,128)S(1)}) custom-call(bf16[32,20480]{1,0:T(8,128)(2,1)} %expression_ref.3, bf16[32,256]{1,0:T(8,128)(2,1)} %current_ref.1, f32[32,64]{1,0:T(8,128)} %covariates_ref.1, s32[2,256]{1,0:T(2,128)} %packed_ref.1), custom_call_target="tpu_custom_call" | custom-call | tf_op jit(solution)/shard_map/pallas_call | solution.py:169
  3.4 23.9 %all-to-all-start = ((bf16[16,32,1024]{2,1,0:T(8,128)(2,1)}), bf16[16,32,1024]{2,1,0:T(8,128)(2,1)S(1)}, u32[]{:S(2)}, u32[]{:S(2)}) async-start(bf16[16,32,1024]{2,1,0:T(8,128)(2,1)} %bitcast.32), calls=%async_computation | async-start | bytes 2097152 | tf_op jit(solution)/shard_map/all_to_all | solution.py:156
  27.3 2.6 %shard_map.61 = bf16[512,640]{1,0:T(8,128)(2,1)} custom-call(bf16[32,20480]{1,0:T(8,128)(2,1)} %expression_ref.3), custom_call_target="tpu_custom_call" | custom-call | tf_op jit(solution)/shard_map/pallas_call | solution.py:169
  29.8 13.4 %all-to-all-done = bf16[16,32,1024]{2,1,0:T(8,128)(2,1)S(1)} async-done(((bf16[16,32,1024]{2,1,0:T(8,128)(2,1)}), bf16[16,32,1024]{2,1,0:T(8,128)(2,1)S(1)}, u32[]{:S(2)}, u32[]{:S(2)}) %all-to-all-start) | async-done | bytes 1048608 | tf_op jit(solution)/shard_map/all_to_all | solution.py:156
  43.2 4.3 %all-to-all-start.1 = ((bf16[16,32,640]{2,1,0:T(8,128)(2,1)}), bf16[16,32,640]{2,1,0:T(8,128)(2,1)S(1)}, u32[]{:S(2)}, u32[]{:S(2)}) async-start(bf16[16,32,640]{2,1,0:T(8,128)(2,1)} %bitcast.31), calls=%async_computation.1 | async-start | bytes 1310720 | tf_op jit(solution)/shard_map/all_to_all | solution.py:156
  47.8 9.3 %collective-permute-start.16 = (s32[8,128]{1,0:T(8,128)S(1)}, s32[8,128]{1,0:T(8,128)S(1)}, u32[]{:S(2)}, u32[]{:S(2)}) collective-permute-start(s32[8,128]{1,0:T(8,128)S(1)} %get-tuple-element.42), channel_id=1, source_target_pairs={{0,48},{16,64},{32,80},{48,96},{64,112},{80,0},{96,16},{112,32},{1... | collective-permute-start | bytes 12296 | tf_op jit(solution)/shard_map/ppermute | solution.py:160
  57.1 2.6 %collective-permute-start.17 = (s32[8,128]{1,0:T(8,128)S(1)}, s32[8,128]{1,0:T(8,128)S(1)}, u32[]{:S(2)}, u32[]{:S(2)}) collective-permute-start(s32[8,128]{1,0:T(8,128)S(1)} %get-tuple-element.41), channel_id=1, source_target_pairs={{0,64},{16,80},{32,96},{48,112},{64,0},{80,16},{96,32},{112,48},{1... | collective-permute-start | bytes 12296 | tf_op jit(solution)/shard_map/ppermute | solution.py:160
  59.7 8.4 %collective-permute-start.18 = (s32[8,128]{1,0:T(8,128)S(1)}, s32[8,128]{1,0:T(8,128)S(1)}, u32[]{:S(2)}, u32[]{:S(2)}) collective-permute-start(s32[8,128]{1,0:T(8,128)S(1)} %get-tuple-element.40), channel_id=1, source_target_pairs={{0,80},{16,96},{32,112},{48,0},{64,16},{80,32},{96,48},{112,64},{1... | collective-permute-start | bytes 12296 | tf_op jit(solution)/shard_map/ppermute | solution.py:160
  69.1 5.4 %collective-permute-done.19.refs_6_ = s32[8,128]{1,0:T(8,128)S(1)} collective-permute-done((s32[8,128]{1,0:T(8,128)S(1)}, s32[8,128]{1,0:T(8,128)S(1)}, u32[]{:S(2)}, u32[]{:S(2)}) %collective-permute-start.19) | collective-permute-done | bytes 4128 | tf_op jit(solution)/shard_map/ppermute | solution.py:160
  74.5 2.0 %shard_map.64.refs_8_ = f32[56,128]{1,0:T(8,128)} custom-call(s32[2]{0:T(128)} %pad_add_fusion.where_ref, bf16[512,1024]{1,0:T(8,128)(2,1)S(1)} %bitcast.24, s32[8,128]{1,0:T(8,128)S(1)} %get-tuple-element.45.refs_0_, s32[8,128]{1,0:T(8,128)S(1)} %collective-permute-done.14.refs_1_, s32[8,128]{1,0:T(8,128)S(1)} %collective-permute-done.15.refs_2_, ...), custom_call_target="tpu_custom_call" | custom-call | tf_op jit(solution)/shard_map/pallas_call | solution.py:169
  76.8 3.3 %collective-permute-start.22 = (f32[56,128]{1,0:T(8,128)}, f32[56,128]{1,0:T(8,128)S(1)}, u32[]{:S(2)}, u32[]{:S(2)}) collective-permute-start(f32[56,128]{1,0:T(8,128)} %shard_map.64.refs_8_), channel_id=1, source_target_pairs={{0,112},{16,0},{32,16},{48,32},{64,48},{80,64},{96,80},{112,96},{1... | collective-permute-start | bytes 86024 | tf_op jit(solution)/shard_map/ppermute | solution.py:160
  80.0 1.5 collective-permute-done.21.refs_9_
  81.5 3.6 %collective-permute-start.24 = (f32[56,128]{1,0:T(8,128)S(1)}, f32[56,128]{1,0:T(8,128)S(1)}, u32[]{:S(2)}, u32[]{:S(2)}) collective-permute-start(f32[56,128]{1,0:T(8,128)S(1)} %collective-permute-done.22.refs_10_), channel_id=1, source_target_pairs={{0,112},{16,0},{32,16},{48,32},{64,48},{80,64},{96,80},{112,96},{1... | collective-permute-start | bytes 86024 | tf_op jit(solution)/shard_map/ppermute | solution.py:160
  85.1 1.3 collective-permute-done.23.refs_11_
  86.3 3.9 %collective-permute-start.26 = (f32[56,128]{1,0:T(8,128)S(1)}, f32[56,128]{1,0:T(8,128)S(1)}, u32[]{:S(2)}, u32[]{:S(2)}) collective-permute-start(f32[56,128]{1,0:T(8,128)S(1)} %collective-permute-done.24.refs_12_), channel_id=1, source_target_pairs={{0,112},{16,0},{32,16},{48,32},{64,48},{80,64},{96,80},{112,96},{1... | collective-permute-start | bytes 86024 | tf_op jit(solution)/shard_map/ppermute | solution.py:160
  90.2 1.3 collective-permute-done.25.refs_13_
  91.6 4.8 %collective-permute-done.27.refs_15_ = f32[56,128]{1,0:T(8,128)S(1)} collective-permute-done((f32[56,128]{1,0:T(8,128)S(1)}, f32[56,128]{1,0:T(8,128)S(1)}, u32[]{:S(2)}, u32[]{:S(2)}) %collective-permute-start.27) | collective-permute-done | bytes 28704 | tf_op jit(solution)/shard_map/ppermute | solution.py:160
  97.1 2.2 %shard_map.65 = bf16[512,256]{1,0:T(8,128)(2,1)} custom-call(s32[2]{0:T(128)} %pad_add_fusion.where_ref, bf16[512,1024]{1,0:T(8,128)(2,1)S(1)} %bitcast.25, s32[8,128]{1,0:T(8,128)S(1)} %get-tuple-element.45.refs_0_, s32[8,128]{1,0:T(8,128)S(1)} %collective-permute-done.14.refs_1_, s32[8,128]{1,0:T(8,128)S(1)} %collective-permute-done.15.refs_2_, ...), custom_call_target="tpu_custom_call" | custom-call | tf_op jit(solution)/shard_map/pallas_call | solution.py:169
  99.3 13.8 %all-to-all-start.2 = ((bf16[16,32,256]{2,1,0:T(8,128)(2,1)}), bf16[16,32,256]{2,1,0:T(8,128)(2,1)S(1)}, u32[]{:S(2)}, u32[]{:S(2)}) async-start(bf16[16,32,256]{2,1,0:T(8,128)(2,1)} %bitcast.33), calls=%async_computation.2 | async-start | bytes 524288 | tf_op jit(solution)/shard_map/all_to_all | solution.py:156
  113.1 1.1 shard_map.62
  114.3 1.1 shard_map.60
  115.4 2.4 %collective-permute-start = (f32[80,256]{1,0:T(8,128)S(1)}, f32[80,256]{1,0:T(8,128)S(1)}, u32[]{:S(2)}, u32[]{:S(2)}) collective-permute-start(f32[80,256]{1,0:T(8,128)S(1)} %get-tuple-element.23), channel_id=1, source_target_pairs={{0,16},{16,32},{32,48},{48,64},{64,80},{80,96},{96,112},{112,0},{1... | collective-permute-start | bytes 245768 | tf_op jit(solution)/shard_map/ppermute | solution.py:160
  117.9 1.2 collective-permute-start.7
  119.1 1.1 collective-permute-start.4
  120.2 2.6 %collective-permute-start.11 = (f32[80,256]{1,0:T(8,128)S(1)}, f32[80,256]{1,0:T(8,128)S(1)}, u32[]{:S(2)}, u32[]{:S(2)}) collective-permute-start(f32[80,256]{1,0:T(8,128)S(1)} %add.108), channel_id=1, source_target_pairs={{0,112},{16,0},{32,16},{48,32},{64,48},{80,64},{96,80},{112,96},{1... | collective-permute-start | bytes 245768 | tf_op jit(solution)/shard_map/ppermute | solution.py:160
  122.8 1.9 %collective-permute-done = f32[80,256]{1,0:T(8,128)S(1)} collective-permute-done((f32[80,256]{1,0:T(8,128)S(1)}, f32[80,256]{1,0:T(8,128)S(1)}, u32[]{:S(2)}, u32[]{:S(2)}) %collective-permute-start) | collective-permute-done | bytes 81952 | tf_op jit(solution)/shard_map/ppermute | solution.py:160
  124.9 3.6 %collective-permute-start.8 = (f32[80,256]{1,0:T(8,128)S(1)}, f32[80,256]{1,0:T(8,128)S(1)}, u32[]{:S(2)}, u32[]{:S(2)}) collective-permute-start(f32[80,256]{1,0:T(8,128)S(1)} %add.106), channel_id=1, source_target_pairs={{0,112},{16,0},{32,16},{48,32},{64,48},{80,64},{96,80},{112,96},{1... | collective-permute-start | bytes 245768 | tf_op jit(solution)/shard_map/ppermute | solution.py:160
  128.7 3.6 %collective-permute-start.12 = (f32[80,256]{1,0:T(8,128)S(1)}, f32[80,256]{1,0:T(8,128)S(1)}, u32[]{:S(2)}, u32[]{:S(2)}) collective-permute-start(f32[80,256]{1,0:T(8,128)S(1)} %add.109), channel_id=1, source_target_pairs={{0,112},{16,0},{32,16},{48,32},{64,48},{80,64},{96,80},{112,96},{1... | collective-permute-start | bytes 245768 | tf_op jit(solution)/shard_map/ppermute | solution.py:160
  132.5 3.6 %collective-permute-start.9 = (f32[80,256]{1,0:T(8,128)S(1)}, f32[80,256]{1,0:T(8,128)S(1)}, u32[]{:S(2)}, u32[]{:S(2)}) collective-permute-start(f32[80,256]{1,0:T(8,128)S(1)} %add.107), channel_id=1, source_target_pairs={{0,112},{16,0},{32,16},{48,32},{64,48},{80,64},{96,80},{112,96},{1... | collective-permute-start | bytes 245768 | tf_op jit(solution)/shard_map/ppermute | solution.py:160
  136.4 3.6 %collective-permute-start.13 = (f32[80,256]{1,0:T(8,128)S(1)}, f32[80,256]{1,0:T(8,128)S(1)}, u32[]{:S(2)}, u32[]{:S(2)}) collective-permute-start(f32[80,256]{1,0:T(8,128)S(1)} %add.110), channel_id=1, source_target_pairs={{0,112},{16,0},{32,16},{48,32},{64,48},{80,64},{96,80},{112,96},{1... | collective-permute-start | bytes 245768 | tf_op jit(solution)/shard_map/ppermute | solution.py:160
  140.2 3.4 %collective-permute-done.6.refs_3_ = f32[80,256]{1,0:T(8,128)S(1)} collective-permute-done((f32[80,256]{1,0:T(8,128)S(1)}, f32[80,256]{1,0:T(8,128)S(1)}, u32[]{:S(2)}, u32[]{:S(2)}) %collective-permute-start.6) | collective-permute-done | bytes 81952 | tf_op jit(solution)/shard_map/ppermute | solution.py:160
  143.6 4.5 %collective-permute-done.3.refs_2_ = f32[80,256]{1,0:T(8,128)S(1)} collective-permute-done((f32[80,256]{1,0:T(8,128)S(1)}, f32[80,256]{1,0:T(8,128)S(1)}, u32[]{:S(2)}, u32[]{:S(2)}) %collective-permute-start.3) | collective-permute-done | bytes 81952 | tf_op jit(solution)/shard_map/ppermute | solution.py:160
  (52 shorter events, 4.6 us)
Async XLA Ops:
  3.4 39.8 %all-to-all-start = ((bf16[16,32,1024]{2,1,0:T(8,128)(2,1)}), bf16[16,32,1024]{2,1,0:T(8,128)(2,1)S(1)}, u32[]{:S(2)}, u32[]{:S(2)}) async-start(bf16[16,32,1024]{2,1,0:T(8,128)(2,1)} %bitcast.32), calls=%async_computation | async-start | bytes 2097152 | tf_op jit(solution)/shard_map/all_to_all | solution.py:156
  43.2 56.1 %all-to-all-start.1 = ((bf16[16,32,640]{2,1,0:T(8,128)(2,1)}), bf16[16,32,640]{2,1,0:T(8,128)(2,1)S(1)}, u32[]{:S(2)}, u32[]{:S(2)}) async-start(bf16[16,32,640]{2,1,0:T(8,128)(2,1)} %bitcast.31), calls=%async_computation.1 | async-start | bytes 1310720 | tf_op jit(solution)/shard_map/all_to_all | solution.py:156
  47.6 20.6 %collective-permute-start.14 = (s32[8,128]{1,0:T(8,128)S(1)}, s32[8,128]{1,0:T(8,128)S(1)}, u32[]{:S(2)}, u32[]{:S(2)}) collective-permute-start(s32[8,128]{1,0:T(8,128)S(1)} %get-tuple-element.44), channel_id=1, source_target_pairs={{0,16},{16,32},{32,48},{48,64},{64,80},{80,96},{96,112},{112,0},{1... | collective-permute-start | bytes 12296 | tf_op jit(solution)/shard_map/ppermute | solution.py:160
  47.7 20.4 %collective-permute-start.15 = (s32[8,128]{1,0:T(8,128)S(1)}, s32[8,128]{1,0:T(8,128)S(1)}, u32[]{:S(2)}, u32[]{:S(2)}) collective-permute-start(s32[8,128]{1,0:T(8,128)S(1)} %get-tuple-element.43), channel_id=1, source_target_pairs={{0,32},{16,48},{32,64},{48,80},{64,96},{80,112},{96,0},{112,16},{1... | collective-permute-start | bytes 12296 | tf_op jit(solution)/shard_map/ppermute | solution.py:160
  47.8 21.2 %collective-permute-start.16 = (s32[8,128]{1,0:T(8,128)S(1)}, s32[8,128]{1,0:T(8,128)S(1)}, u32[]{:S(2)}, u32[]{:S(2)}) collective-permute-start(s32[8,128]{1,0:T(8,128)S(1)} %get-tuple-element.42), channel_id=1, source_target_pairs={{0,48},{16,64},{32,80},{48,96},{64,112},{80,0},{96,16},{112,32},{1... | collective-permute-start | bytes 12296 | tf_op jit(solution)/shard_map/ppermute | solution.py:160
  57.1 11.9 %collective-permute-start.17 = (s32[8,128]{1,0:T(8,128)S(1)}, s32[8,128]{1,0:T(8,128)S(1)}, u32[]{:S(2)}, u32[]{:S(2)}) collective-permute-start(s32[8,128]{1,0:T(8,128)S(1)} %get-tuple-element.41), channel_id=1, source_target_pairs={{0,64},{16,80},{32,96},{48,112},{64,0},{80,16},{96,32},{112,48},{1... | collective-permute-start | bytes 12296 | tf_op jit(solution)/shard_map/ppermute | solution.py:160
  59.7 9.3 %collective-permute-start.18 = (s32[8,128]{1,0:T(8,128)S(1)}, s32[8,128]{1,0:T(8,128)S(1)}, u32[]{:S(2)}, u32[]{:S(2)}) collective-permute-start(s32[8,128]{1,0:T(8,128)S(1)} %get-tuple-element.40), channel_id=1, source_target_pairs={{0,80},{16,96},{32,112},{48,0},{64,16},{80,32},{96,48},{112,64},{1... | collective-permute-start | bytes 12296 | tf_op jit(solution)/shard_map/ppermute | solution.py:160
  68.1 6.4 %collective-permute-start.19 = (s32[8,128]{1,0:T(8,128)S(1)}, s32[8,128]{1,0:T(8,128)S(1)}, u32[]{:S(2)}, u32[]{:S(2)}) collective-permute-start(s32[8,128]{1,0:T(8,128)S(1)} %get-tuple-element.39), channel_id=1, source_target_pairs={{0,96},{16,112},{32,0},{48,16},{64,32},{80,48},{96,64},{112,80},{1... | collective-permute-start | bytes 12296 | tf_op jit(solution)/shard_map/ppermute | solution.py:160
  68.1 6.4 %collective-permute-start.20 = (s32[8,128]{1,0:T(8,128)S(1)}, s32[8,128]{1,0:T(8,128)S(1)}, u32[]{:S(2)}, u32[]{:S(2)}) collective-permute-start(s32[8,128]{1,0:T(8,128)S(1)} %get-tuple-element.38), channel_id=1, source_target_pairs={{0,112},{16,0},{32,16},{48,32},{64,48},{80,64},{96,80},{112,96},{1... | collective-permute-start | bytes 12296 | tf_op jit(solution)/shard_map/ppermute | solution.py:160
  76.5 5.0 %collective-permute-start.21 = (f32[56,128]{1,0:T(8,128)}, f32[56,128]{1,0:T(8,128)S(1)}, u32[]{:S(2)}, u32[]{:S(2)}) collective-permute-start(f32[56,128]{1,0:T(8,128)} %shard_map.64.refs_8_), channel_id=1, source_target_pairs={{0,16},{16,32},{32,48},{48,64},{64,80},{80,96},{96,112},{112,0},{1... | collective-permute-start | bytes 86024 | tf_op jit(solution)/shard_map/ppermute | solution.py:160
  76.8 4.7 %collective-permute-start.22 = (f32[56,128]{1,0:T(8,128)}, f32[56,128]{1,0:T(8,128)S(1)}, u32[]{:S(2)}, u32[]{:S(2)}) collective-permute-start(f32[56,128]{1,0:T(8,128)} %shard_map.64.refs_8_), channel_id=1, source_target_pairs={{0,112},{16,0},{32,16},{48,32},{64,48},{80,64},{96,80},{112,96},{1... | collective-permute-start | bytes 86024 | tf_op jit(solution)/shard_map/ppermute | solution.py:160
  81.5 4.8 %collective-permute-start.23 = (f32[56,128]{1,0:T(8,128)S(1)}, f32[56,128]{1,0:T(8,128)S(1)}, u32[]{:S(2)}, u32[]{:S(2)}) collective-permute-start(f32[56,128]{1,0:T(8,128)S(1)} %collective-permute-done.21.refs_9_), channel_id=1, source_target_pairs={{0,16},{16,32},{32,48},{48,64},{64,80},{80,96},{96,112},{112,0},{1... | collective-permute-start | bytes 86024 | tf_op jit(solution)/shard_map/ppermute | solution.py:160
  81.5 4.8 %collective-permute-start.24 = (f32[56,128]{1,0:T(8,128)S(1)}, f32[56,128]{1,0:T(8,128)S(1)}, u32[]{:S(2)}, u32[]{:S(2)}) collective-permute-start(f32[56,128]{1,0:T(8,128)S(1)} %collective-permute-done.22.refs_10_), channel_id=1, source_target_pairs={{0,112},{16,0},{32,16},{48,32},{64,48},{80,64},{96,80},{112,96},{1... | collective-permute-start | bytes 86024 | tf_op jit(solution)/shard_map/ppermute | solution.py:160
  86.3 5.2 %collective-permute-start.25 = (f32[56,128]{1,0:T(8,128)S(1)}, f32[56,128]{1,0:T(8,128)S(1)}, u32[]{:S(2)}, u32[]{:S(2)}) collective-permute-start(f32[56,128]{1,0:T(8,128)S(1)} %collective-permute-done.23.refs_11_), channel_id=1, source_target_pairs={{0,16},{16,32},{32,48},{48,64},{64,80},{80,96},{96,112},{112,0},{1... | collective-permute-start | bytes 86024 | tf_op jit(solution)/shard_map/ppermute | solution.py:160
  86.3 5.2 %collective-permute-start.26 = (f32[56,128]{1,0:T(8,128)S(1)}, f32[56,128]{1,0:T(8,128)S(1)}, u32[]{:S(2)}, u32[]{:S(2)}) collective-permute-start(f32[56,128]{1,0:T(8,128)S(1)} %collective-permute-done.24.refs_12_), channel_id=1, source_target_pairs={{0,112},{16,0},{32,16},{48,32},{64,48},{80,64},{96,80},{112,96},{1... | collective-permute-start | bytes 86024 | tf_op jit(solution)/shard_map/ppermute | solution.py:160
  91.5 4.8 %collective-permute-start.27 = (f32[56,128]{1,0:T(8,128)S(1)}, f32[56,128]{1,0:T(8,128)S(1)}, u32[]{:S(2)}, u32[]{:S(2)}) collective-permute-start(f32[56,128]{1,0:T(8,128)S(1)} %collective-permute-done.25.refs_13_), channel_id=1, source_target_pairs={{0,16},{16,32},{32,48},{48,64},{64,80},{80,96},{96,112},{112,0},{1... | collective-permute-start | bytes 86024 | tf_op jit(solution)/shard_map/ppermute | solution.py:160
  96.4 0.7 copy-start
  99.3 49.4 %all-to-all-start.2 = ((bf16[16,32,256]{2,1,0:T(8,128)(2,1)}), bf16[16,32,256]{2,1,0:T(8,128)(2,1)S(1)}, u32[]{:S(2)}, u32[]{:S(2)}) async-start(bf16[16,32,256]{2,1,0:T(8,128)(2,1)} %bitcast.33), calls=%async_computation.2 | async-start | bytes 524288 | tf_op jit(solution)/shard_map/all_to_all | solution.py:156
  114.2 6.1 %collective-permute-start.10 = (f32[80,256]{1,0:T(8,128)S(1)}, f32[80,256]{1,0:T(8,128)S(1)}, u32[]{:S(2)}, u32[]{:S(2)}) collective-permute-start(f32[80,256]{1,0:T(8,128)S(1)} %get-tuple-element.33), channel_id=1, source_target_pairs={{0,112},{16,0},{32,16},{48,32},{64,48},{80,64},{96,80},{112,96},{1... | collective-permute-start | bytes 245768 | tf_op jit(solution)/shard_map/ppermute | solution.py:160
  115.4 9.3 %collective-permute-start = (f32[80,256]{1,0:T(8,128)S(1)}, f32[80,256]{1,0:T(8,128)S(1)}, u32[]{:S(2)}, u32[]{:S(2)}) collective-permute-start(f32[80,256]{1,0:T(8,128)S(1)} %get-tuple-element.23), channel_id=1, source_target_pairs={{0,16},{16,32},{32,48},{48,64},{64,80},{80,96},{96,112},{112,0},{1... | collective-permute-start | bytes 245768 | tf_op jit(solution)/shard_map/ppermute | solution.py:160
  117.9 7.0 %collective-permute-start.7 = (f32[80,256]{1,0:T(8,128)S(1)}, f32[80,256]{1,0:T(8,128)S(1)}, u32[]{:S(2)}, u32[]{:S(2)}) collective-permute-start(f32[80,256]{1,0:T(8,128)S(1)} %get-tuple-element.30), channel_id=1, source_target_pairs={{0,112},{16,0},{32,16},{48,32},{64,48},{80,64},{96,80},{112,96},{1... | collective-permute-start | bytes 245768 | tf_op jit(solution)/shard_map/ppermute | solution.py:160
  119.1 9.4 %collective-permute-start.4 = (f32[80,256]{1,0:T(8,128)S(1)}, f32[80,256]{1,0:T(8,128)S(1)}, u32[]{:S(2)}, u32[]{:S(2)}) collective-permute-start(f32[80,256]{1,0:T(8,128)S(1)} %get-tuple-element.27), channel_id=1, source_target_pairs={{0,16},{16,32},{32,48},{48,64},{64,80},{80,96},{96,112},{112,0},{1... | collective-permute-start | bytes 245768 | tf_op jit(solution)/shard_map/ppermute | solution.py:160
  120.2 8.4 %collective-permute-start.11 = (f32[80,256]{1,0:T(8,128)S(1)}, f32[80,256]{1,0:T(8,128)S(1)}, u32[]{:S(2)}, u32[]{:S(2)}) collective-permute-start(f32[80,256]{1,0:T(8,128)S(1)} %add.108), channel_id=1, source_target_pairs={{0,112},{16,0},{32,16},{48,32},{64,48},{80,64},{96,80},{112,96},{1... | collective-permute-start | bytes 245768 | tf_op jit(solution)/shard_map/ppermute | solution.py:160
  124.7 7.7 %collective-permute-start.1 = (f32[80,256]{1,0:T(8,128)S(1)}, f32[80,256]{1,0:T(8,128)S(1)}, u32[]{:S(2)}, u32[]{:S(2)}) collective-permute-start(f32[80,256]{1,0:T(8,128)S(1)} %add.101), channel_id=1, source_target_pairs={{0,16},{16,32},{32,48},{48,64},{64,80},{80,96},{96,112},{112,0},{1... | collective-permute-start | bytes 245768 | tf_op jit(solution)/shard_map/ppermute | solution.py:160
  124.9 7.6 %collective-permute-start.8 = (f32[80,256]{1,0:T(8,128)S(1)}, f32[80,256]{1,0:T(8,128)S(1)}, u32[]{:S(2)}, u32[]{:S(2)}) collective-permute-start(f32[80,256]{1,0:T(8,128)S(1)} %add.106), channel_id=1, source_target_pairs={{0,112},{16,0},{32,16},{48,32},{64,48},{80,64},{96,80},{112,96},{1... | collective-permute-start | bytes 245768 | tf_op jit(solution)/shard_map/ppermute | solution.py:160
  128.5 7.7 %collective-permute-start.5 = (f32[80,256]{1,0:T(8,128)S(1)}, f32[80,256]{1,0:T(8,128)S(1)}, u32[]{:S(2)}, u32[]{:S(2)}) collective-permute-start(f32[80,256]{1,0:T(8,128)S(1)} %add.104), channel_id=1, source_target_pairs={{0,16},{16,32},{32,48},{48,64},{64,80},{80,96},{96,112},{112,0},{1... | collective-permute-start | bytes 245768 | tf_op jit(solution)/shard_map/ppermute | solution.py:160
  128.7 7.6 %collective-permute-start.12 = (f32[80,256]{1,0:T(8,128)S(1)}, f32[80,256]{1,0:T(8,128)S(1)}, u32[]{:S(2)}, u32[]{:S(2)}) collective-permute-start(f32[80,256]{1,0:T(8,128)S(1)} %add.109), channel_id=1, source_target_pairs={{0,112},{16,0},{32,16},{48,32},{64,48},{80,64},{96,80},{112,96},{1... | collective-permute-start | bytes 245768 | tf_op jit(solution)/shard_map/ppermute | solution.py:160
  132.4 7.7 %collective-permute-start.2 = (f32[80,256]{1,0:T(8,128)S(1)}, f32[80,256]{1,0:T(8,128)S(1)}, u32[]{:S(2)}, u32[]{:S(2)}) collective-permute-start(f32[80,256]{1,0:T(8,128)S(1)} %add.102), channel_id=1, source_target_pairs={{0,16},{16,32},{32,48},{48,64},{64,80},{80,96},{96,112},{112,0},{1... | collective-permute-start | bytes 245768 | tf_op jit(solution)/shard_map/ppermute | solution.py:160
  132.5 7.6 %collective-permute-start.9 = (f32[80,256]{1,0:T(8,128)S(1)}, f32[80,256]{1,0:T(8,128)S(1)}, u32[]{:S(2)}, u32[]{:S(2)}) collective-permute-start(f32[80,256]{1,0:T(8,128)S(1)} %add.107), channel_id=1, source_target_pairs={{0,112},{16,0},{32,16},{48,32},{64,48},{80,64},{96,80},{112,96},{1... | collective-permute-start | bytes 245768 | tf_op jit(solution)/shard_map/ppermute | solution.py:160
  136.2 7.4 %collective-permute-start.6 = (f32[80,256]{1,0:T(8,128)S(1)}, f32[80,256]{1,0:T(8,128)S(1)}, u32[]{:S(2)}, u32[]{:S(2)}) collective-permute-start(f32[80,256]{1,0:T(8,128)S(1)} %add.105), channel_id=1, source_target_pairs={{0,16},{16,32},{32,48},{48,64},{64,80},{80,96},{96,112},{112,0},{1... | collective-permute-start | bytes 245768 | tf_op jit(solution)/shard_map/ppermute | solution.py:160
  136.4 7.2 %collective-permute-start.13 = (f32[80,256]{1,0:T(8,128)S(1)}, f32[80,256]{1,0:T(8,128)S(1)}, u32[]{:S(2)}, u32[]{:S(2)}) collective-permute-start(f32[80,256]{1,0:T(8,128)S(1)} %add.110), channel_id=1, source_target_pairs={{0,112},{16,0},{32,16},{48,32},{64,48},{80,64},{96,80},{112,96},{1... | collective-permute-start | bytes 245768 | tf_op jit(solution)/shard_map/ppermute | solution.py:160
  140.0 8.0 %collective-permute-start.3 = (f32[80,256]{1,0:T(8,128)S(1)}, f32[80,256]{1,0:T(8,128)S(1)}, u32[]{:S(2)}, u32[]{:S(2)}) collective-permute-start(f32[80,256]{1,0:T(8,128)S(1)} %add.103), channel_id=1, source_target_pairs={{0,16},{16,32},{32,48},{48,64},{64,80},{80,96},{96,112},{112,0},{1... | collective-permute-start | bytes 245768 | tf_op jit(solution)/shard_map/ppermute | solution.py:160

commit v2 on v0

v2 whole, which is shorter than its diff:
```python
import functools

import jax
import jax.numpy as jnp
from jax import lax
from jax.experimental import pallas as pl
from jax.experimental.pallas import tpu as pltpu
from jax.sharding import Mesh
from jax.sharding import PartitionSpec as P

RING = 8
LOCAL = 16
SPEC = P(("parts", "q", "p", "c"), None)
NEAR = ("p", "c")
F32 = jnp.float32
BF16 = jnp.bfloat16
HIGHEST = lax.Precision.HIGHEST
WORD = 16
PIECES = RING // 2 + 2
ROOM = pltpu.CompilerParams(vmem_limit_bytes=16 * 2**20)


def core():
    return lax.axis_index("c")


def position():
    return lax.axis_index("q")


def one_hot(hits):
    return hits.astype(F32).astype(BF16)


def dot(left, right, dims, precision=None):
    return lax.dot_general(
        left, right, (dims, ((), ())), precision=precision, preferred_element_type=F32
    )


def prepare_kernel(expression_ref, current_ref, covariates_ref, out_ref):
    rows, genes = expression_ref.shape
    block = genes // RING
    share = block // LOCAL
    half = share // 2
    far = RING // 2
    around = []
    for ahead in range(RING):
        at = pl.multiple_of(lax.rem(position() + ahead, RING) * block, 128)
        around.append(expression_ref[:, pl.ds(at, block)])
    cov = covariates_ref[...]
    high = cov.astype(BF16)
    low = (cov - high.astype(F32)).astype(BF16)
    own = [current_ref[...], high, low]
    for j in range(LOCAL):
        way = 1 - 2 * (j % 2)
        pieces = []
        for target in (j ^ 1, j):
            at = target * share + (j % 2) * half
            pieces.append(around[far][:, at : at + half])
        for distance in range(far - 1, 0, -1):
            for target in (j ^ 1, j):
                at = target * share
                halves = [
                    around[way * distance % RING][:, at + part * half : at + (part + 1) * half]
                    for part in (j % 2, 1 - j % 2)
                ]
                pieces += halves
        pieces.append(around[0][:, j * share : (j + 1) * share])
        out_ref[j * rows : (j + 1) * rows, :] = jnp.concatenate(pieces + own, axis=1)


def words_kernel(mine_ref, given_ref, out_ref):
    held, words = mine_ref.shape
    split = words // RING
    first = core() == 0
    mine, given = mine_ref[...], given_ref[...]
    both = jnp.concatenate(
        [jnp.where(first, mine, given), jnp.where(first, given, mine)], axis=0
    )
    out_ref[...] = jnp.zeros_like(out_ref)
    for q in range(RING):
        out_ref[q * 8 : q * 8 + 2 * held, 0:split] = both[:, q * split : (q + 1) * split]


def product_kernel(genes, variants, rows_ref, *refs):
    whole = dot(rows_ref[:, :genes], rows_ref[:, genes : genes + variants], ((0,), (0,)))
    refs[0][...] = rows_ref[:, genes + variants :]
    at = 0
    for ref in refs[1:]:
        ref[...] = whole[at : at + ref.shape[0], :]
        at += ref.shape[0]


def merge_kernel(block_ref, come_ref, out_ref):
    half = come_ref.shape[0]
    out_ref[0:half, :] = block_ref[0:half, :] + come_ref[...]
    out_ref[half:, :] = block_ref[half:, :]


def total_kernel(scale, own_ref, mine_ref, given_ref, out_ref):
    half = own_ref.shape[0] // 2
    here = core()
    for part in range(2):
        rows = slice(part * half, (part + 1) * half)
        mine = mine_ref[pl.ds((here ^ part) * half, half), :]
        given = given_ref[pl.ds((here ^ part ^ 1) * half, half), :]
        out_ref[rows, :] = (own_ref[rows, :] + mine + given) * scale


def unpack(word_refs, held, share):
    rows = [ref[at : at + held, 0:share] for ref in word_refs for at in range(0, ref.shape[0], 8)]
    words = jnp.concatenate(rows, axis=0)
    wide = jnp.concatenate([words] * 4, axis=1)
    lane = lax.broadcasted_iota(jnp.int32, wide.shape, 1)
    octets = (lax.shift_right_logical(wide, 8 * (lane // share)) & 255).astype(F32).astype(BF16)
    count = RING * held
    row = lax.broadcasted_iota(jnp.int32, (count, count), 0)
    col = lax.broadcasted_iota(jnp.int32, (count, count), 1)
    behind = (position() - row // held) * (1 - 2 * core()) % RING
    slot = jnp.where(behind <= RING // 2, behind, RING + RING // 2 - behind)
    order = (col // held == slot) & (col % held == row % held)
    octets = dot(order.astype(F32).astype(BF16), octets, ((1,), (0,))).astype(BF16)
    samples = share * WORD
    row = lax.broadcasted_iota(jnp.int32, (4 * share, samples), 0)
    col = lax.broadcasted_iota(jnp.int32, (4 * share, samples), 1)
    pick = (row % share == col // WORD) & (row // share == (col % WORD) // 4)
    spread = dot(octets, pick.astype(F32).astype(BF16), ((1,), (0,))).astype(jnp.int32)
    place = lax.broadcasted_iota(jnp.int32, spread.shape, 1)
    return (lax.shift_right_logical(spread, 2 * (place % 4)) & 3).astype(F32)


def covariate_terms(rows_ref, covs):
    return [rows_ref[:, k * covs : (k + 1) * covs] for k in range(2)]


def stats_kernel(held, share, covs, rows_ref, *refs):
    out_ref = refs[PIECES]
    dosage = unpack(refs[:PIECES], held, share)
    count, samples = dosage.shape
    ones = jnp.ones((8, samples), F32)
    wide = jnp.concatenate([dosage, ones], axis=0)
    exact = wide.astype(BF16)
    terms = covariate_terms(rows_ref, covs)
    projected = sum(dot(exact, term, ((1,), (0,))) for term in reversed(terms))
    half = covs // 2
    height = count + 8 + half
    cov = sum(term.astype(F32) for term in reversed(terms))
    gram = dot(cov, cov, ((0,), (0,)), HIGHEST)
    counted = jnp.sum(wide, axis=1, keepdims=True)
    squares = jnp.sum(wide * wide, axis=1, keepdims=True)
    pad = jnp.zeros((count + 8, covs - 2), F32)
    table = jnp.concatenate([projected, counted, squares, pad], axis=1)
    lower = jnp.concatenate([gram[0:half], gram[half:]], axis=1)
    out_ref[0 : count + 8, :] = table
    out_ref[count + 8 : height, :] = lower


def one_way_kernel(*refs):
    last = jnp.where(core() == 0, refs[-2][...], 0.0)
    refs[-1][...] = sum((ref[...] for ref in refs[:-2]), last)


def finish_kernel(held, share, variants, covs, total, rows_ref, *refs):
    out_ref, placed_ref = refs[-2:]
    dosage = unpack(refs[:PIECES], held, share)
    count, _ = dosage.shape
    half = covs // 2
    table = refs[PIECES][...]
    for ref in refs[PIECES + 1 : -2]:
        table = table + ref[...]
    gram = jnp.concatenate(
        [
            table[count + 8 : count + 8 + half, 0:covs],
            table[count + 8 : count + 8 + half, covs : 2 * covs],
        ],
        axis=0,
    )
    projected = table[0:count, 0:covs]
    cov_sums = table[count : count + 1, 0:covs]
    counted = table[0:count, covs : covs + 1]
    squares = table[0:count, covs + 1 : covs + 2]
    average = counted / total
    loading = projected - average * cov_sums
    through = dot(loading, gram, ((1,), (0,)), HIGHEST)
    sq_norm = (
        squares
        - counted * average
        + jnp.sum(loading * (through - 2.0 * loading), axis=1, keepdims=True)
    )
    cov = sum(term.astype(F32) for term in reversed(covariate_terms(rows_ref, covs)))
    leftover = dosage - average - dot(loading, cov, ((1,), (1,)), HIGHEST)
    scaled = (leftover * lax.rsqrt(sq_norm / total + 1e-05)).astype(BF16)
    row = lax.broadcasted_iota(jnp.int32, (count, variants), 0)
    col = lax.broadcasted_iota(jnp.int32, (count, variants), 1)
    target = (row // held) * (held * LOCAL // 2) + lax.axis_index("p") * held + row % held
    placed_ref[...] = dot(scaled, one_hot(col == target), ((0,), (0,)))
    share_rows = scaled.shape[1] // LOCAL
    for peer in range(LOCAL // 2):
        first = pl.multiple_of((2 * peer + core()) * share_rows, share_rows)
        out_ref[peer * share_rows : (peer + 1) * share_rows, :] = placed_ref[
            pl.ds(first, share_rows), :
        ].astype(BF16)


def exchange(array, axis):
    return lax.all_to_all(array, axis, split_axis=0, concat_axis=0, tiled=True)


def hop(array, steps=1):
    pairs = [
        (2 * k + side, 2 * ((k + steps * (1 - 2 * side)) % RING) + side)
        for k in range(RING)
        for side in range(2)
    ]
    return lax.ppermute(array, ("q", "c"), pairs)


def swap(array):
    return lax.ppermute(array, "c", [(0, 1), (1, 0)])


def kernel(body, out_shape, given=(), scratch=()):
    specs = [pl.BlockSpec(memory_space=space) for space in given]

    def call(*operands):
        rest = operands[len(specs) :]
        held = [pltpu.with_memory_space_constraint(array, pltpu.VMEM) for array in rest]
        return pl.pallas_call(
            body,
            out_shape=out_shape,
            compiler_params=None if given else ROOM,
            in_specs=specs + [pl.BlockSpec(memory_space=pltpu.VMEM)] * len(held),
            scratch_shapes=scratch,
        )(*operands[: len(specs)], *held)

    return call


def block_step(expression, current, next_packed, covariates):
    rows, genes = expression.shape
    variants = current.shape[1]
    covs = covariates.shape[1]
    held, words = 2 * next_packed.shape[0], next_packed.shape[1]
    share = words // RING
    total = rows * RING * LOCAL
    own_genes = genes // (RING * LOCAL)
    q = lax.axis_index("q")

    count = RING * held
    height = count + 8 + covs // 2
    local_genes = genes // LOCAL
    at = local_genes + variants
    moved = kernel(
        prepare_kernel, jax.ShapeDtypeStruct((LOCAL * rows, at + 2 * covs), BF16), [pltpu.VMEM] * 3
    )(expression, current, covariates)
    moved = exchange(moved, NEAR)
    packed = kernel(
        words_kernel, pltpu.VMEM((RING * 8, 128), jnp.int32), [pltpu.VMEM]
    )(next_packed, swap(next_packed))
    packed = packed.reshape(RING, 8, 128)
    far = RING // 2
    way = 1 - 2 * lax.axis_index("c")
    mine = []
    for distance in range(1, far + 1):
        piece = lax.dynamic_index_in_dim(
            packed, (q + way * distance + RING) % RING, 0, keepdims=False
        )
        mine.append(hop(piece, distance))
    given = swap(jnp.concatenate(mine[:-1], axis=0))
    pieces = [lax.dynamic_index_in_dim(packed, q, 0, keepdims=False), *mine, given]

    heights = [own_genes // 2] * 2 + [own_genes] * (2 * far - 1)
    terms, *blocks = kernel(
        functools.partial(product_kernel, local_genes, variants),
        [pltpu.VMEM((LOCAL * rows, 2 * covs), BF16)]
        + [pltpu.VMEM((height, variants), F32) for height in heights[:-1]]
        + [jax.ShapeDtypeStruct((own_genes, variants), F32)],
    )(moved)

    stats = kernel(
        functools.partial(stats_kernel, held, share, covs),
        jax.ShapeDtypeStruct((height, 2 * covs), F32),
    )(terms, *pieces)
    passed = []
    ahead = stats
    for _ in range(1, RING // 2 + 1):
        ahead = hop(ahead)
        passed.append(ahead)
    one_way = kernel(one_way_kernel, pltpu.VMEM((height, 2 * covs), F32))(*passed)
    sums = [stats, one_way, swap(one_way)]
    placed = kernel(
        functools.partial(finish_kernel, held, share, variants, covs, float(total)),
        jax.ShapeDtypeStruct((LOCAL // 2 * rows, variants), BF16),
        scratch=[pltpu.VMEM((LOCAL * rows, variants), F32)],
    )(terms, *pieces, *sums)
    placed = exchange(placed, "p")
    next_block = jnp.sum(placed.reshape(-1, rows, variants).astype(F32), axis=0).astype(BF16)

    scale_factor = float(total) ** (-0.5)
    merged = pltpu.VMEM((own_genes, variants), F32)
    away, same = hop(blocks[0]), hop(blocks[1])
    away = hop(kernel(merge_kernel, merged)(blocks[2], away))
    same = hop(kernel(merge_kernel, merged)(blocks[3], same))
    for step in range(3, far + 1):
        away = hop(blocks[2 * step - 2] + away)
        same = hop(blocks[2 * step - 1] + same)
    given = swap(away)
    scores = kernel(
        functools.partial(total_kernel, scale_factor),
        jax.ShapeDtypeStruct((own_genes, variants), F32),
    )(blocks[-1], same, given)
    return (scores, next_block)


def solution(mesh):
    split = Mesh(mesh.devices.reshape(mesh.shape["parts"], RING, LOCAL // 2, 2), ("parts", "q", "p", "c"))
    return jax.shard_map(
        block_step, mesh=split, in_specs=(SPEC,) * 4, out_specs=(SPEC,) * 2, check_vma=False
    )
```

time: 131 us -> 126 us (0.962)
  waiting for transfers between devices: 17.7 us -> 49.8 us
  starting transfers between devices: 97.4 us -> 65.9 us
  local copies, waits for them, and re-layouts: 3.42 us -> 0.01 us
  Pallas kernels: 9.14 us -> 7.44 us
    ppermute x28 -> x20, starting transfers between devices: 58.4 us -> 38 us  [the longest x16 29.6 us: hop(): return lax.ppermute(array, ('q', 'c'), pairs)]
    all_to_all x2, waiting for transfers between devices: 0.01 us -> 16.3 us  [exchange(): return lax.all_to_all(array, axis, split_axis=0, concat_axis=0, tiled=True)]
    ppermute x28 -> x20, waiting for transfers between devices: 17.7 us -> 33.5 us  [the longest x16 32.7 us: hop(): return lax.ppermute(array, ('q', 'c'), pairs)]
    all_to_all x2, starting transfers between devices: 38.9 us -> 27.9 us  [exchange(): return lax.all_to_all(array, axis, split_axis=0, concat_axis=0, tiled=True)]
    unnamed x6 -> x2, local copies, waits for them, and re-layouts: 3.41 us -> 0.01 us
    pallas_call x5 -> x9, Pallas kernels: 9.14 us -> 7.44 us  [call(): pl.pallas_call(body, out_shape=out_shape, compiler_params=None if given e...]
  transfers between devices with their start and end apart: 30 -> 22, of which waited for: 12 -> 11; matrix products, arithmetic and copies ran while one was open for 1% -> 1% of each run, Pallas kernels for 2% -> 3%
where the time goes in v2:
time: 126 us; the launch traced here: 125 us
  starting transfers between devices  65.9 us (52%)
  waiting for transfers between devices  49.8 us (40%)
  Pallas kernels  7.44 us (6%)
    ppermute x16, waiting for transfers between devices, hop(): return lax.ppermute(array, ('q', 'c'), pairs)  32.7 us
    ppermute x16, starting transfers between devices, hop(): return lax.ppermute(array, ('q', 'c'), pairs)  29.6 us
    all_to_all x2, starting transfers between devices, exchange(): return lax.all_to_all(array, axis, split_axis=0, concat_axis=0, tiled=True)  27.9 us
    all_to_all x2, waiting for transfers between devices, exchange(): return lax.all_to_all(array, axis, split_axis=0, concat_axis=0, tiled=True)  16.3 us
    ppermute x4, starting transfers between devices, swap(): return lax.ppermute(array, 'c', [(0, 1), (1, 0)])  8.44 us
    pallas_call x9, Pallas kernels, call(): pl.pallas_call(body, out_shape=out_shape, compiler_params=None if given e...  7.44 us
  transfers between devices with their start and end apart: 22, of which 11 were waited for; matrix products, arithmetic and copies ran while one was open for 1% of the time, Pallas kernels for 3%

profile of v2, /device:TPU:33, one launch (start us, length us, event | category | flops | bytes accessed | tf_op | source)
XLA Modules:
  0.0 124.6 jit_solution(7993438544094930811)
XLA Ops:
  0.6 3.1 %shard_map.59 = bf16[512,1664]{1,0:T(8,128)(2,1)} custom-call(bf16[32,20480]{1,0:T(8,128)(2,1)} %expression_ref.1, bf16[32,256]{1,0:T(8,128)(2,1)} %current_ref.1, f32[32,64]{1,0:T(8,128)} %covariates_ref.1), custom_call_target="tpu_custom_call" | custom-call | tf_op jit(solution)/shard_map/pallas_call | solution.py:229
  3.8 24.1 %all-to-all-start = ((bf16[16,32,1664]{2,1,0:T(8,128)(2,1)}), bf16[16,32,1664]{2,1,0:T(8,128)(2,1)S(1)}, u32[]{:S(2)}, u32[]{:S(2)}) async-start(bf16[16,32,1664]{2,1,0:T(8,128)(2,1)} %bitcast.16), calls=%async_computation | async-start | bytes 3407872 | tf_op jit(solution)/shard_map/all_to_all | solution.py:207
  27.8 0.8 collective-permute-start.9
  28.6 0.8 collective-permute-done.9.given_ref
  29.4 0.8 shard_map.64
  30.2 4.9 %collective-permute-start.10 = (s32[8,128]{1,0:T(8,128)S(1)}, s32[8,128]{1,0:T(8,128)S(1)}, u32[]{:S(2)}, u32[]{:S(2)}) collective-permute-start(s32[8,128]{1,0:T(8,128)S(1)} %get-tuple-element.25), channel_id=1, source_target_pairs={{0,16},{1,113},{16,32},{17,1},{32,48},{33,17},{48,64},{49,33},{64,... | collective-permute-start | bytes 12296 | tf_op jit(solution)/shard_map/ppermute | solution.py:216
  35.1 16.3 %all-to-all-done = bf16[16,32,1664]{2,1,0:T(8,128)(2,1)S(1)} async-done(((bf16[16,32,1664]{2,1,0:T(8,128)(2,1)}), bf16[16,32,1664]{2,1,0:T(8,128)(2,1)S(1)}, u32[]{:S(2)}, u32[]{:S(2)}) %all-to-all-start) | async-done | bytes 1703968 | tf_op jit(solution)/shard_map/all_to_all | solution.py:207
  51.3 0.6 shard_map.60
  51.9 5.1 %collective-permute-start.4 = (f32[80,256]{1,0:T(8,128)S(1)}, f32[80,256]{1,0:T(8,128)S(1)}, u32[]{:S(2)}, u32[]{:S(2)}) collective-permute-start(f32[80,256]{1,0:T(8,128)S(1)} %get-tuple-element.20), channel_id=1, source_target_pairs={{0,16},{1,113},{16,32},{17,1},{32,48},{33,17},{48,64},{49,33},{64,... | collective-permute-start | bytes 245768 | tf_op jit(solution)/shard_map/ppermute | solution.py:216
  57.2 1.6 %collective-permute-done.4.come_ref = f32[80,256]{1,0:T(8,128)S(1)} collective-permute-done((f32[80,256]{1,0:T(8,128)S(1)}, f32[80,256]{1,0:T(8,128)S(1)}, u32[]{:S(2)}, u32[]{:S(2)}) %collective-permute-start.4) | collective-permute-done | bytes 81952 | tf_op jit(solution)/shard_map/ppermute | solution.py:216
  58.8 4.1 %collective-permute-start.5 = (f32[160,256]{1,0:T(8,128)S(1)}, f32[160,256]{1,0:T(8,128)S(1)}, u32[]{:S(2)}, u32[]{:S(2)}) collective-permute-start(f32[160,256]{1,0:T(8,128)S(1)} %shard_map.62), channel_id=1, source_target_pairs={{0,16},{1,113},{16,32},{17,1},{32,48},{33,17},{48,64},{49,33},{64,... | collective-permute-start | bytes 491528 | tf_op jit(solution)/shard_map/ppermute | solution.py:216
  62.9 11.2 %collective-permute-done.13.refs_4_ = s32[8,128]{1,0:T(8,128)S(1)} collective-permute-done((s32[8,128]{1,0:T(8,128)S(1)}, s32[8,128]{1,0:T(8,128)S(1)}, u32[]{:S(2)}, u32[]{:S(2)}) %collective-permute-start.13) | collective-permute-done | bytes 4128 | tf_op jit(solution)/shard_map/ppermute | solution.py:216
  74.1 0.7 shard_map.65.refs_6_
  74.8 0.2 collective-permute-start.15
  75.0 3.6 %collective-permute-done.15.refs_0_ = f32[72,128]{1,0:T(8,128)S(1)} collective-permute-done((f32[72,128]{1,0:T(8,128)S(1)}, f32[72,128]{1,0:T(8,128)S(1)}, u32[]{:S(2)}, u32[]{:S(2)}) %collective-permute-start.15) | collective-permute-done | bytes 36896 | tf_op jit(solution)/shard_map/ppermute | solution.py:216
  78.6 1.4 %collective-permute-start.16 = (f32[72,128]{1,0:T(8,128)S(1)}, f32[72,128]{1,0:T(8,128)S(1)}, u32[]{:S(2)}, u32[]{:S(2)}) collective-permute-start(f32[72,128]{1,0:T(8,128)S(1)} %collective-permute-done.15.refs_0_), channel_id=1, source_target_pairs={{0,16},{1,113},{16,32},{17,1},{32,48},{33,17},{48,64},{49,33},{64,... | collective-permute-start | bytes 110600 | tf_op jit(solution)/shard_map/ppermute | solution.py:216
  80.0 2.3 %collective-permute-done.16.refs_1_ = f32[72,128]{1,0:T(8,128)S(1)} collective-permute-done((f32[72,128]{1,0:T(8,128)S(1)}, f32[72,128]{1,0:T(8,128)S(1)}, u32[]{:S(2)}, u32[]{:S(2)}) %collective-permute-start.16) | collective-permute-done | bytes 36896 | tf_op jit(solution)/shard_map/ppermute | solution.py:216
  82.3 3.0 %collective-permute-start.17 = (f32[72,128]{1,0:T(8,128)S(1)}, f32[72,128]{1,0:T(8,128)S(1)}, u32[]{:S(2)}, u32[]{:S(2)}) collective-permute-start(f32[72,128]{1,0:T(8,128)S(1)} %collective-permute-done.16.refs_1_), channel_id=1, source_target_pairs={{0,16},{1,113},{16,32},{17,1},{32,48},{33,17},{48,64},{49,33},{64,... | collective-permute-start | bytes 110600 | tf_op jit(solution)/shard_map/ppermute | solution.py:216
  85.3 1.1 collective-permute-done.17.refs_2_
  86.4 3.9 %collective-permute-start.18 = (f32[72,128]{1,0:T(8,128)S(1)}, f32[72,128]{1,0:T(8,128)S(1)}, u32[]{:S(2)}, u32[]{:S(2)}) collective-permute-start(f32[72,128]{1,0:T(8,128)S(1)} %collective-permute-done.17.refs_2_), channel_id=1, source_target_pairs={{0,16},{1,113},{16,32},{17,1},{32,48},{33,17},{48,64},{49,33},{64,... | collective-permute-start | bytes 110600 | tf_op jit(solution)/shard_map/ppermute | solution.py:216
  90.2 1.1 collective-permute-done.18.refs_3_
  91.3 7.5 %collective-permute-start.19 = (f32[72,128]{1,0:T(8,128)S(1)}, f32[72,128]{1,0:T(8,128)S(1)}, u32[]{:S(2)}, u32[]{:S(2)}) collective-permute-start(f32[72,128]{1,0:T(8,128)S(1)} %shard_map.66.refs_7_), channel_id=1, source_target_pairs={{0,1},{1,0},{2,3},{3,2},{4,5},{5,4},{6,7},{7,6},{8,9},{9,8},{10,11... | collective-permute-start | bytes 110600 | tf_op jit(solution)/shard_map/ppermute | solution.py:220
  98.9 1.3 %collective-permute-start.1 = (f32[160,256]{1,0:T(8,128)S(1)}, f32[160,256]{1,0:T(8,128)S(1)}, u32[]{:S(2)}, u32[]{:S(2)}) collective-permute-start(f32[160,256]{1,0:T(8,128)S(1)} %shard_map.61), channel_id=1, source_target_pairs={{0,16},{1,113},{16,32},{17,1},{32,48},{33,17},{48,64},{49,33},{64,... | collective-permute-start | bytes 491528 | tf_op jit(solution)/shard_map/ppermute | solution.py:216
  100.2 4.0 %collective-permute-start.6 = (f32[160,256]{1,0:T(8,128)S(1)}, f32[160,256]{1,0:T(8,128)S(1)}, u32[]{:S(2)}, u32[]{:S(2)}) collective-permute-start(f32[160,256]{1,0:T(8,128)S(1)} %add.67), channel_id=1, source_target_pairs={{0,16},{1,113},{16,32},{17,1},{32,48},{33,17},{48,64},{49,33},{64,... | collective-permute-start | bytes 491528 | tf_op jit(solution)/shard_map/ppermute | solution.py:216
  104.2 1.6 %shard_map.67 = bf16[256,256]{1,0:T(8,128)(2,1)} custom-call(bf16[512,128]{1,0:T(8,128)(2,1)S(1)} %get-tuple-element.21.rows_ref, s32[8,128]{1,0:T(8,128)S(1)} %get-tuple-element.26.refs_0_, s32[8,128]{1,0:T(8,128)S(1)} %collective-permute-done.10.refs_1_, s32[8,128]{1,0:T(8,128)S(1)} %collective-permute-done.11.refs_2_, ...), custom_call_target="tpu_custom_call" | custom-call | tf_op jit(solution)/shard_map/pallas_call | solution.py:229
  105.7 3.8 %all-to-all-start.1 = ((bf16[8,32,256]{2,1,0:T(8,128)(2,1)}), bf16[8,32,256]{2,1,0:T(8,128)(2,1)S(1)}, u32[]{:S(2)}, u32[]{:S(2)}) async-start(bf16[8,32,256]{2,1,0:T(8,128)(2,1)} %bitcast.8), calls=%async_computation.1 | async-start | bytes 262144 | tf_op jit(solution)/shard_map/all_to_all | solution.py:207
  109.7 1.5 %collective-permute-start.7 = (f32[160,256]{1,0:T(8,128)S(1)}, f32[160,256]{1,0:T(8,128)S(1)}, u32[]{:S(2)}, u32[]{:S(2)}) collective-permute-start(f32[160,256]{1,0:T(8,128)S(1)} %add.68), channel_id=1, source_target_pairs={{0,16},{1,113},{16,32},{17,1},{32,48},{33,17},{48,64},{49,33},{64,... | collective-permute-start | bytes 491528 | tf_op jit(solution)/shard_map/ppermute | solution.py:216
  111.2 5.8 %collective-permute-done.2 = f32[160,256]{1,0:T(8,128)S(1)} collective-permute-done((f32[160,256]{1,0:T(8,128)S(1)}, f32[160,256]{1,0:T(8,128)S(1)}, u32[]{:S(2)}, u32[]{:S(2)}) %collective-permute-start.2) | collective-permute-done | bytes 163872 | tf_op jit(solution)/shard_map/ppermute | solution.py:216
  117.2 2.9 %collective-permute-done.7 = f32[160,256]{1,0:T(8,128)S(1)} collective-permute-done((f32[160,256]{1,0:T(8,128)S(1)}, f32[160,256]{1,0:T(8,128)S(1)}, u32[]{:S(2)}, u32[]{:S(2)}) %collective-permute-start.7) | collective-permute-done | bytes 163872 | tf_op jit(solution)/shard_map/ppermute | solution.py:216
  120.1 0.6 reduce_sum.12
  120.7 3.2 %collective-permute-done.3.mine_ref = f32[160,256]{1,0:T(8,128)S(1)} collective-permute-done((f32[160,256]{1,0:T(8,128)S(1)}, f32[160,256]{1,0:T(8,128)S(1)}, u32[]{:S(2)}, u32[]{:S(2)}) %collective-permute-start.3) | collective-permute-done | bytes 163872 | tf_op jit(solution)/shard_map/ppermute | solution.py:216
  123.9 0.7 shard_map.63
  (30 shorter events, 0.6 us)
Async XLA Ops:
  3.8 24.1 %copy-start = (s32[2,256]{1,0:T(2,128)S(1)}, s32[2,256]{1,0:T(2,128)}, u32[]{:S(2)}) copy-start(s32[2,256]{1,0:T(2,128)} %mine_ref.1) | copy-start | bytes 6148
  3.8 47.6 %all-to-all-start = ((bf16[16,32,1664]{2,1,0:T(8,128)(2,1)}), bf16[16,32,1664]{2,1,0:T(8,128)(2,1)S(1)}, u32[]{:S(2)}, u32[]{:S(2)}) async-start(bf16[16,32,1664]{2,1,0:T(8,128)(2,1)} %bitcast.16), calls=%async_computation | async-start | bytes 3407872 | tf_op jit(solution)/shard_map/all_to_all | solution.py:207
  27.8 1.6 %collective-permute-start.9 = (s32[2,256]{1,0:T(2,128)S(1)}, s32[2,256]{1,0:T(2,128)S(1)}, u32[]{:S(2)}, u32[]{:S(2)}) collective-permute-start(s32[2,256]{1,0:T(2,128)S(1)} %copy-done), channel_id=1, source_target_pairs={{0,1},{1,0},{2,3},{3,2},{4,5},{5,4},{6,7},{7,6},{8,9},{9,8},{10,11... | collective-permute-start | bytes 6152 | tf_op jit(solution)/shard_map/ppermute | solution.py:220
  30.2 26.8 %collective-permute-start.10 = (s32[8,128]{1,0:T(8,128)S(1)}, s32[8,128]{1,0:T(8,128)S(1)}, u32[]{:S(2)}, u32[]{:S(2)}) collective-permute-start(s32[8,128]{1,0:T(8,128)S(1)} %get-tuple-element.25), channel_id=1, source_target_pairs={{0,16},{1,113},{16,32},{17,1},{32,48},{33,17},{48,64},{49,33},{64,... | collective-permute-start | bytes 12296 | tf_op jit(solution)/shard_map/ppermute | solution.py:216
  35.1 21.9 %collective-permute-start.11 = (s32[8,128]{1,0:T(8,128)S(1)}, s32[8,128]{1,0:T(8,128)S(1)}, u32[]{:S(2)}, u32[]{:S(2)}) collective-permute-start(s32[8,128]{1,0:T(8,128)S(1)} %get-tuple-element.24), channel_id=1, source_target_pairs={{0,32},{1,97},{16,48},{17,113},{32,64},{33,1},{48,80},{49,17},{64,... | collective-permute-start | bytes 12296 | tf_op jit(solution)/shard_map/ppermute | solution.py:216
  35.1 21.9 %collective-permute-start.12 = (s32[8,128]{1,0:T(8,128)S(1)}, s32[8,128]{1,0:T(8,128)S(1)}, u32[]{:S(2)}, u32[]{:S(2)}) collective-permute-start(s32[8,128]{1,0:T(8,128)S(1)} %get-tuple-element.23), channel_id=1, source_target_pairs={{0,48},{1,81},{16,64},{17,97},{32,80},{33,113},{48,96},{49,1},{64,... | collective-permute-start | bytes 12296 | tf_op jit(solution)/shard_map/ppermute | solution.py:216
  51.9 6.9 %collective-permute-start.4 = (f32[80,256]{1,0:T(8,128)S(1)}, f32[80,256]{1,0:T(8,128)S(1)}, u32[]{:S(2)}, u32[]{:S(2)}) collective-permute-start(f32[80,256]{1,0:T(8,128)S(1)} %get-tuple-element.20), channel_id=1, source_target_pairs={{0,16},{1,113},{16,32},{17,1},{32,48},{33,17},{48,64},{49,33},{64,... | collective-permute-start | bytes 245768 | tf_op jit(solution)/shard_map/ppermute | solution.py:216
  57.0 17.1 %collective-permute-start.14 = (s32[24,128]{1,0:T(8,128)S(1)}, s32[24,128]{1,0:T(8,128)S(1)}, u32[]{:S(2)}, u32[]{:S(2)}) collective-permute-start(s32[24,128]{1,0:T(8,128)S(1)} %pad_add_fusion), channel_id=1, source_target_pairs={{0,1},{1,0},{2,3},{3,2},{4,5},{5,4},{6,7},{7,6},{8,9},{9,8},{10,11... | collective-permute-start | bytes 36872 | tf_op jit(solution)/shard_map/ppermute | solution.py:220
  58.8 41.4 %collective-permute-start.5 = (f32[160,256]{1,0:T(8,128)S(1)}, f32[160,256]{1,0:T(8,128)S(1)}, u32[]{:S(2)}, u32[]{:S(2)}) collective-permute-start(f32[160,256]{1,0:T(8,128)S(1)} %shard_map.62), channel_id=1, source_target_pairs={{0,16},{1,113},{16,32},{17,1},{32,48},{33,17},{48,64},{49,33},{64,... | collective-permute-start | bytes 491528 | tf_op jit(solution)/shard_map/ppermute | solution.py:216
  62.9 11.2 %collective-permute-start.13 = (s32[8,128]{1,0:T(8,128)S(1)}, s32[8,128]{1,0:T(8,128)S(1)}, u32[]{:S(2)}, u32[]{:S(2)}) collective-permute-start(s32[8,128]{1,0:T(8,128)S(1)} %get-tuple-element.22), channel_id=1, source_target_pairs={{0,64},{1,65},{16,80},{17,81},{32,96},{33,97},{48,112},{49,113},{6... | collective-permute-start | bytes 12296 | tf_op jit(solution)/shard_map/ppermute | solution.py:216
  74.8 3.8 %collective-permute-start.15 = (f32[72,128]{1,0:T(8,128)S(1)}, f32[72,128]{1,0:T(8,128)S(1)}, u32[]{:S(2)}, u32[]{:S(2)}) collective-permute-start(f32[72,128]{1,0:T(8,128)S(1)} %shard_map.65.refs_6_), channel_id=1, source_target_pairs={{0,16},{1,113},{16,32},{17,1},{32,48},{33,17},{48,64},{49,33},{64,... | collective-permute-start | bytes 110600 | tf_op jit(solution)/shard_map/ppermute | solution.py:216
  78.6 3.7 %collective-permute-start.16 = (f32[72,128]{1,0:T(8,128)S(1)}, f32[72,128]{1,0:T(8,128)S(1)}, u32[]{:S(2)}, u32[]{:S(2)}) collective-permute-start(f32[72,128]{1,0:T(8,128)S(1)} %collective-permute-done.15.refs_0_), channel_id=1, source_target_pairs={{0,16},{1,113},{16,32},{17,1},{32,48},{33,17},{48,64},{49,33},{64,... | collective-permute-start | bytes 110600 | tf_op jit(solution)/shard_map/ppermute | solution.py:216
  79.9 18.9 %collective-permute-start = (f32[80,256]{1,0:T(8,128)S(1)}, f32[80,256]{1,0:T(8,128)S(1)}, u32[]{:S(2)}, u32[]{:S(2)}) collective-permute-start(f32[80,256]{1,0:T(8,128)S(1)} %get-tuple-element.16), channel_id=1, source_target_pairs={{0,16},{1,113},{16,32},{17,1},{32,48},{33,17},{48,64},{49,33},{64,... | collective-permute-start | bytes 245768 | tf_op jit(solution)/shard_map/ppermute | solution.py:216
  82.3 4.1 %collective-permute-start.17 = (f32[72,128]{1,0:T(8,128)S(1)}, f32[72,128]{1,0:T(8,128)S(1)}, u32[]{:S(2)}, u32[]{:S(2)}) collective-permute-start(f32[72,128]{1,0:T(8,128)S(1)} %collective-permute-done.16.refs_1_), channel_id=1, source_target_pairs={{0,16},{1,113},{16,32},{17,1},{32,48},{33,17},{48,64},{49,33},{64,... | collective-permute-start | bytes 110600 | tf_op jit(solution)/shard_map/ppermute | solution.py:216
  86.4 4.9 %collective-permute-start.18 = (f32[72,128]{1,0:T(8,128)S(1)}, f32[72,128]{1,0:T(8,128)S(1)}, u32[]{:S(2)}, u32[]{:S(2)}) collective-permute-start(f32[72,128]{1,0:T(8,128)S(1)} %collective-permute-done.17.refs_2_), channel_id=1, source_target_pairs={{0,16},{1,113},{16,32},{17,1},{32,48},{33,17},{48,64},{49,33},{64,... | collective-permute-start | bytes 110600 | tf_op jit(solution)/shard_map/ppermute | solution.py:216
  91.3 12.9 %collective-permute-start.19 = (f32[72,128]{1,0:T(8,128)S(1)}, f32[72,128]{1,0:T(8,128)S(1)}, u32[]{:S(2)}, u32[]{:S(2)}) collective-permute-start(f32[72,128]{1,0:T(8,128)S(1)} %shard_map.66.refs_7_), channel_id=1, source_target_pairs={{0,1},{1,0},{2,3},{3,2},{4,5},{5,4},{6,7},{7,6},{8,9},{9,8},{10,11... | collective-permute-start | bytes 110600 | tf_op jit(solution)/shard_map/ppermute | solution.py:220
  98.9 10.7 %collective-permute-start.1 = (f32[160,256]{1,0:T(8,128)S(1)}, f32[160,256]{1,0:T(8,128)S(1)}, u32[]{:S(2)}, u32[]{:S(2)}) collective-permute-start(f32[160,256]{1,0:T(8,128)S(1)} %shard_map.61), channel_id=1, source_target_pairs={{0,16},{1,113},{16,32},{17,1},{32,48},{33,17},{48,64},{49,33},{64,... | collective-permute-start | bytes 491528 | tf_op jit(solution)/shard_map/ppermute | solution.py:216
  100.2 9.5 %collective-permute-start.6 = (f32[160,256]{1,0:T(8,128)S(1)}, f32[160,256]{1,0:T(8,128)S(1)}, u32[]{:S(2)}, u32[]{:S(2)}) collective-permute-start(f32[160,256]{1,0:T(8,128)S(1)} %add.67), channel_id=1, source_target_pairs={{0,16},{1,113},{16,32},{17,1},{32,48},{33,17},{48,64},{49,33},{64,... | collective-permute-start | bytes 491528 | tf_op jit(solution)/shard_map/ppermute | solution.py:216
  105.7 14.3 %all-to-all-start.1 = ((bf16[8,32,256]{2,1,0:T(8,128)(2,1)}), bf16[8,32,256]{2,1,0:T(8,128)(2,1)S(1)}, u32[]{:S(2)}, u32[]{:S(2)}) async-start(bf16[8,32,256]{2,1,0:T(8,128)(2,1)} %bitcast.8), calls=%async_computation.1 | async-start | bytes 262144 | tf_op jit(solution)/shard_map/all_to_all | solution.py:207
  109.6 7.4 %collective-permute-start.2 = (f32[160,256]{1,0:T(8,128)S(1)}, f32[160,256]{1,0:T(8,128)S(1)}, u32[]{:S(2)}, u32[]{:S(2)}) collective-permute-start(f32[160,256]{1,0:T(8,128)S(1)} %add.65), channel_id=1, source_target_pairs={{0,16},{1,113},{16,32},{17,1},{32,48},{33,17},{48,64},{49,33},{64,... | collective-permute-start | bytes 491528 | tf_op jit(solution)/shard_map/ppermute | solution.py:216
  109.7 10.3 %collective-permute-start.7 = (f32[160,256]{1,0:T(8,128)S(1)}, f32[160,256]{1,0:T(8,128)S(1)}, u32[]{:S(2)}, u32[]{:S(2)}) collective-permute-start(f32[160,256]{1,0:T(8,128)S(1)} %add.68), channel_id=1, source_target_pairs={{0,16},{1,113},{16,32},{17,1},{32,48},{33,17},{48,64},{49,33},{64,... | collective-permute-start | bytes 491528 | tf_op jit(solution)/shard_map/ppermute | solution.py:216
  117.0 6.8 %collective-permute-start.3 = (f32[160,256]{1,0:T(8,128)S(1)}, f32[160,256]{1,0:T(8,128)S(1)}, u32[]{:S(2)}, u32[]{:S(2)}) collective-permute-start(f32[160,256]{1,0:T(8,128)S(1)} %add.66), channel_id=1, source_target_pairs={{0,16},{1,113},{16,32},{17,1},{32,48},{33,17},{48,64},{49,33},{64,... | collective-permute-start | bytes 491528 | tf_op jit(solution)/shard_map/ppermute | solution.py:216
  120.1 3.8 %collective-permute-start.8 = (f32[160,256]{1,0:T(8,128)S(1)}, f32[160,256]{1,0:T(8,128)S(1)}, u32[]{:S(2)}, u32[]{:S(2)}) collective-permute-start(f32[160,256]{1,0:T(8,128)S(1)} %collective-permute-done.7), channel_id=1, source_target_pairs={{0,1},{1,0},{2,3},{3,2},{4,5},{5,4},{6,7},{7,6},{8,9},{9,8},{10,11... | collective-permute-start | bytes 491528 | tf_op jit(solution)/shard_map/ppermute | solution.py:220

commit v3 on v2

--- a/solution.py
+++ b/solution.py
@@ -16,7 +16,6 @@
 BF16 = jnp.bfloat16
 HIGHEST = lax.Precision.HIGHEST
 WORD = 16
-PIECES = RING // 2 + 2
 ROOM = pltpu.CompilerParams(vmem_limit_bytes=16 * 2**20)
 
 
@@ -61,11 +60,12 @@
         for distance in range(far - 1, 0, -1):
             for target in (j ^ 1, j):
                 at = target * share
-                halves = [
-                    around[way * distance % RING][:, at + part * half : at + (part + 1) * half]
-                    for part in (j % 2, 1 - j % 2)
-                ]
-                pieces += halves
+                there = around[way * distance % RING]
+                cuts = ((at, at + half), (at + half, at + share))
+                if j % 2:
+                    pieces += [there[:, first:last] for first, last in reversed(cuts)]
+                else:
+                    pieces.append(there[:, at : at + share])
         pieces.append(around[0][:, j * share : (j + 1) * share])
         out_ref[j * rows : (j + 1) * rows, :] = jnp.concatenate(pieces + own, axis=1)
 
@@ -109,17 +109,15 @@
 
 
 def unpack(word_refs, held, share):
-    rows = [ref[at : at + held, 0:share] for ref in word_refs for at in range(0, ref.shape[0], 8)]
-    words = jnp.concatenate(rows, axis=0)
+    words = jnp.concatenate([ref[0:held, 0:share] for ref in word_refs], axis=0)
     wide = jnp.concatenate([words] * 4, axis=1)
     lane = lax.broadcasted_iota(jnp.int32, wide.shape, 1)
     octets = (lax.shift_right_logical(wide, 8 * (lane // share)) & 255).astype(F32).astype(BF16)
     count = RING * held
     row = lax.broadcasted_iota(jnp.int32, (count, count), 0)
     col = lax.broadcasted_iota(jnp.int32, (count, count), 1)
-    behind = (position() - row // held) * (1 - 2 * core()) % RING
-    slot = jnp.where(behind <= RING // 2, behind, RING + RING // 2 - behind)
-    order = (col // held == slot) & (col % held == row % held)
+    behind = (position() + RING - row // held) % RING
+    order = (col // held == behind) & (col % held == row % held)
     octets = dot(order.astype(F32).astype(BF16), octets, ((1,), (0,))).astype(BF16)
     samples = share * WORD
     row = lax.broadcasted_iota(jnp.int32, (4 * share, samples), 0)
@@ -135,8 +133,8 @@
 
 
 def stats_kernel(held, share, covs, rows_ref, *refs):
-    out_ref = refs[PIECES]
-    dosage = unpack(refs[:PIECES], held, share)
+    out_ref = refs[RING]
+    dosage = unpack(refs[:RING], held, share)
     count, samples = dosage.shape
     ones = jnp.ones((8, samples), F32)
     wide = jnp.concatenate([dosage, ones], axis=0)
@@ -163,11 +161,11 @@
 
 def finish_kernel(held, share, variants, covs, total, rows_ref, *refs):
     out_ref, placed_ref = refs[-2:]
-    dosage = unpack(refs[:PIECES], held, share)
+    dosage = unpack(refs[:RING], held, share)
     count, _ = dosage.shape
     half = covs // 2
-    table = refs[PIECES][...]
-    for ref in refs[PIECES + 1 : -2]:
+    table = refs[RING][...]
+    for ref in refs[RING + 1 : -2]:
         table = table + ref[...]
     gram = jnp.concatenate(
         [
@@ -207,11 +205,15 @@
     return lax.all_to_all(array, axis, split_axis=0, concat_axis=0, tiled=True)
 
 
-def hop(array, steps=1):
+def shift(array, by):
+    return lax.ppermute(array, "q", [(k, (k + by) % RING) for k in range(RING)])
+
+
+def hop(array):
     pairs = [
-        (2 * k + side, 2 * ((k + steps * (1 - 2 * side)) % RING) + side)
+        (2 * k + core, 2 * ((k + 1 - 2 * core) % RING) + core)
         for k in range(RING)
-        for side in range(2)
+        for core in range(2)
     ]
     return lax.ppermute(array, ("q", "c"), pairs)
 
@@ -259,17 +261,12 @@
         words_kernel, pltpu.VMEM((RING * 8, 128), jnp.int32), [pltpu.VMEM]
     )(next_packed, swap(next_packed))
     packed = packed.reshape(RING, 8, 128)
+    pieces = []
+    for ahead in range(RING):
+        piece = lax.dynamic_index_in_dim(packed, (q + ahead) % RING, 0, keepdims=False)
+        pieces.append(shift(piece, ahead) if ahead else piece)
+
     far = RING // 2
-    way = 1 - 2 * lax.axis_index("c")
-    mine = []
-    for distance in range(1, far + 1):
-        piece = lax.dynamic_index_in_dim(
-            packed, (q + way * distance + RING) % RING, 0, keepdims=False
-        )
-        mine.append(hop(piece, distance))
-    given = swap(jnp.concatenate(mine[:-1], axis=0))
-    pieces = [lax.dynamic_index_in_dim(packed, q, 0, keepdims=False), *mine, given]
-
     heights = [own_genes // 2] * 2 + [own_genes] * (2 * far - 1)
     terms, *blocks = kernel(
         functools.partial(product_kernel, local_genes, variants),

time: 126 us -> 142 us (1.13)
  the two profiles are of different devices: /device:TPU:33 before, /device:TPU:164 now
where the time goes in v3:
time: 142 us; the launch traced here: 141 us
  waiting for transfers between devices  46.7 us (33%)
  starting transfers between devices  43.7 us (31%)
  blocking collectives  42.1 us (30%)
  Pallas kernels  7.42 us (5%)
    all_to_all x1, blocking collectives, exchange(): return lax.all_to_all(array, axis, split_axis=0, concat_axis=0, tiled=True)  42.1 us
    ppermute x12, waiting for transfers between devices, hop(): return lax.ppermute(array, ('q', 'c'), pairs)  41.3 us
    ppermute x7, starting transfers between devices, shift(): return lax.ppermute(array, 'q', [(k, (k + by) % RING) for k in range(RING)])  24.2 us
    ppermute x12, starting transfers between devices, hop(): return lax.ppermute(array, ('q', 'c'), pairs)  8.64 us
    pallas_call x9, Pallas kernels, call(): pl.pallas_call(body, out_shape=out_shape, compiler_params=None if given e...  7.42 us
    all_to_all x1, starting transfers between devices, exchange(): return lax.all_to_all(array, axis, split_axis=0, concat_axis=0, tiled=True)  5.72 us
    ppermute x3, starting transfers between devices, swap(): return lax.ppermute(array, 'c', [(0, 1), (1, 0)])  5.21 us
    ppermute x7, waiting for transfers between devices, shift(): return lax.ppermute(array, 'q', [(k, (k + by) % RING) for k in range(RING)])  4.54 us
  transfers between devices with their start and end apart: 23, of which 12 were waited for; matrix products, arithmetic and copies ran while one was open for 1% of the time, Pallas kernels for 2%

profile of v3, /device:TPU:164, one launch (start us, length us, event | category | flops | bytes accessed | tf_op | source)
XLA Modules:
  0.0 141.4 jit_solution(8208831821379179711)
XLA Ops:
  0.6 3.1 %shard_map.59 = bf16[512,1664]{1,0:T(8,128)(2,1)} custom-call(bf16[32,20480]{1,0:T(8,128)(2,1)} %expression_ref.1, bf16[32,256]{1,0:T(8,128)(2,1)} %current_ref.1, f32[32,64]{1,0:T(8,128)} %covariates_ref.1), custom_call_target="tpu_custom_call" | custom-call | tf_op jit(solution)/shard_map/pallas_call | solution.py:231
  3.8 42.1 %all_to_all.20 = bf16[16,32,1664]{2,1,0:T(8,128)(2,1)S(1)} all-to-all(bf16[16,32,1664]{2,1,0:T(8,128)(2,1)} %bitcast.22), channel_id=1, replica_groups=mesh['parts'=2,'q'=8,'p'=8,'c'=2] {'p','c'}, dimensions={0} | all-to-all | bytes 3407872 | tf_op jit(solution)/shard_map/all_to_all | solution.py:205
  45.8 0.6 shard_map.60
  46.5 5.1 %collective-permute-start.9 = (s32[2,256]{1,0:T(2,128)S(1)}, s32[2,256]{1,0:T(2,128)S(1)}, u32[]{:S(2)}, u32[]{:S(2)}) collective-permute-start(s32[2,256]{1,0:T(2,128)S(1)} %copy-done), channel_id=1, source_target_pairs={{0,1},{1,0},{2,3},{3,2},{4,5},{5,4},{6,7},{7,6},{8,9},{9,8},{10,11... | collective-permute-start | bytes 6152 | tf_op jit(solution)/shard_map/ppermute | solution.py:222
  51.6 0.8 collective-permute-done.9.given_ref
  52.4 0.8 shard_map.64
  53.2 1.9 %collective-permute-done.4.come_ref = f32[80,256]{1,0:T(8,128)S(1)} collective-permute-done((f32[80,256]{1,0:T(8,128)S(1)}, f32[80,256]{1,0:T(8,128)S(1)}, u32[]{:S(2)}, u32[]{:S(2)}) %collective-permute-start.4) | collective-permute-done | bytes 81952 | tf_op jit(solution)/shard_map/ppermute | solution.py:218
  55.4 3.9 %collective-permute-start.11 = (s32[8,128]{1,0:T(8,128)S(1)}, s32[8,128]{1,0:T(8,128)S(1)}, u32[]{:S(2)}, u32[]{:S(2)}) collective-permute-start(s32[8,128]{1,0:T(8,128)S(1)} %get-tuple-element.27), channel_id=1, source_target_pairs={{0,32},{16,48},{32,64},{48,80},{64,96},{80,112},{96,0},{112,16},{1... | collective-permute-start | bytes 12296 | tf_op jit(solution)/shard_map/ppermute | solution.py:209
  59.3 6.4 %collective-permute-start.12 = (s32[8,128]{1,0:T(8,128)S(1)}, s32[8,128]{1,0:T(8,128)S(1)}, u32[]{:S(2)}, u32[]{:S(2)}) collective-permute-start(s32[8,128]{1,0:T(8,128)S(1)} %get-tuple-element.26), channel_id=1, source_target_pairs={{0,48},{16,64},{32,80},{48,96},{64,112},{80,0},{96,16},{112,32},{1... | collective-permute-start | bytes 12296 | tf_op jit(solution)/shard_map/ppermute | solution.py:209
  65.7 1.5 %collective-permute-start.13 = (s32[8,128]{1,0:T(8,128)S(1)}, s32[8,128]{1,0:T(8,128)S(1)}, u32[]{:S(2)}, u32[]{:S(2)}) collective-permute-start(s32[8,128]{1,0:T(8,128)S(1)} %get-tuple-element.25), channel_id=1, source_target_pairs={{0,64},{16,80},{32,96},{48,112},{64,0},{80,16},{96,32},{112,48},{1... | collective-permute-start | bytes 12296 | tf_op jit(solution)/shard_map/ppermute | solution.py:209
  67.2 8.9 %collective-permute-start.14 = (s32[8,128]{1,0:T(8,128)S(1)}, s32[8,128]{1,0:T(8,128)S(1)}, u32[]{:S(2)}, u32[]{:S(2)}) collective-permute-start(s32[8,128]{1,0:T(8,128)S(1)} %get-tuple-element.24), channel_id=1, source_target_pairs={{0,80},{16,96},{32,112},{48,0},{64,16},{80,32},{96,48},{112,64},{1... | collective-permute-start | bytes 12296 | tf_op jit(solution)/shard_map/ppermute | solution.py:209
  76.1 3.3 %collective-permute-start.15 = (s32[8,128]{1,0:T(8,128)S(1)}, s32[8,128]{1,0:T(8,128)S(1)}, u32[]{:S(2)}, u32[]{:S(2)}) collective-permute-start(s32[8,128]{1,0:T(8,128)S(1)} %get-tuple-element.23), channel_id=1, source_target_pairs={{0,96},{16,112},{32,0},{48,16},{64,32},{80,48},{96,64},{112,80},{1... | collective-permute-start | bytes 12296 | tf_op jit(solution)/shard_map/ppermute | solution.py:209
  79.5 4.3 %collective-permute-done.15.refs_6_ = s32[8,128]{1,0:T(8,128)S(1)} collective-permute-done((s32[8,128]{1,0:T(8,128)S(1)}, s32[8,128]{1,0:T(8,128)S(1)}, u32[]{:S(2)}, u32[]{:S(2)}) %collective-permute-start.15) | collective-permute-done | bytes 4128 | tf_op jit(solution)/shard_map/ppermute | solution.py:209
  83.8 0.2 collective-permute-done.16.refs_7_
  84.0 0.7 shard_map.65.refs_8_
  84.7 1.2 collective-permute-start.17
  85.9 5.1 %collective-permute-done.17.refs_0_ = f32[72,128]{1,0:T(8,128)S(1)} collective-permute-done((f32[72,128]{1,0:T(8,128)S(1)}, f32[72,128]{1,0:T(8,128)S(1)}, u32[]{:S(2)}, u32[]{:S(2)}) %collective-permute-start.17) | collective-permute-done | bytes 36896 | tf_op jit(solution)/shard_map/ppermute | solution.py:218
  91.0 3.0 %collective-permute-start = (f32[80,256]{1,0:T(8,128)S(1)}, f32[80,256]{1,0:T(8,128)S(1)}, u32[]{:S(2)}, u32[]{:S(2)}) collective-permute-start(f32[80,256]{1,0:T(8,128)S(1)} %get-tuple-element.16), channel_id=1, source_target_pairs={{0,16},{1,113},{16,32},{17,1},{32,48},{33,17},{48,64},{49,33},{64,... | collective-permute-start | bytes 245768 | tf_op jit(solution)/shard_map/ppermute | solution.py:218
  94.0 3.1 %collective-permute-done.18.refs_1_ = f32[72,128]{1,0:T(8,128)S(1)} collective-permute-done((f32[72,128]{1,0:T(8,128)S(1)}, f32[72,128]{1,0:T(8,128)S(1)}, u32[]{:S(2)}, u32[]{:S(2)}) %collective-permute-start.18) | collective-permute-done | bytes 36896 | tf_op jit(solution)/shard_map/ppermute | solution.py:218
  97.1 6.3 %collective-permute-done.19.refs_2_ = f32[72,128]{1,0:T(8,128)S(1)} collective-permute-done((f32[72,128]{1,0:T(8,128)S(1)}, f32[72,128]{1,0:T(8,128)S(1)}, u32[]{:S(2)}, u32[]{:S(2)}) %collective-permute-start.19) | collective-permute-done | bytes 36896 | tf_op jit(solution)/shard_map/ppermute | solution.py:218
  103.4 6.3 %collective-permute-done.20.refs_3_ = f32[72,128]{1,0:T(8,128)S(1)} collective-permute-done((f32[72,128]{1,0:T(8,128)S(1)}, f32[72,128]{1,0:T(8,128)S(1)}, u32[]{:S(2)}, u32[]{:S(2)}) %collective-permute-start.20) | collective-permute-done | bytes 36896 | tf_op jit(solution)/shard_map/ppermute | solution.py:218
  110.1 3.6 %collective-permute-start.6 = (f32[160,256]{1,0:T(8,128)S(1)}, f32[160,256]{1,0:T(8,128)S(1)}, u32[]{:S(2)}, u32[]{:S(2)}) collective-permute-start(f32[160,256]{1,0:T(8,128)S(1)} %add.85), channel_id=1, source_target_pairs={{0,16},{1,113},{16,32},{17,1},{32,48},{33,17},{48,64},{49,33},{64,... | collective-permute-start | bytes 491528 | tf_op jit(solution)/shard_map/ppermute | solution.py:218
  113.7 1.5 %shard_map.67 = bf16[256,256]{1,0:T(8,128)(2,1)} custom-call(bf16[512,128]{1,0:T(8,128)(2,1)S(1)} %get-tuple-element.21.rows_ref, s32[8,128]{1,0:T(8,128)S(1)} %get-tuple-element.29.refs_0_, s32[8,128]{1,0:T(8,128)S(1)} %collective-permute-done.10.refs_1_, s32[8,128]{1,0:T(8,128)S(1)} %collective-permute-done.11.refs_2_, ...), custom_call_target="tpu_custom_call" | custom-call | tf_op jit(solution)/shard_map/pallas_call | solution.py:231
  115.2 5.7 %all-to-all-start.1 = ((bf16[8,32,256]{2,1,0:T(8,128)(2,1)}), bf16[8,32,256]{2,1,0:T(8,128)(2,1)S(1)}, u32[]{:S(2)}, u32[]{:S(2)}) async-start(bf16[8,32,256]{2,1,0:T(8,128)(2,1)} %bitcast.11), calls=%async_computation.1 | async-start | bytes 262144 | tf_op jit(solution)/shard_map/all_to_all | solution.py:205
  121.0 0.1 collective-permute-start.2
  121.1 1.3 collective-permute-done.6
  122.4 0.2 collective-permute-start.7
  122.6 9.4 %collective-permute-done.2 = f32[160,256]{1,0:T(8,128)S(1)} collective-permute-done((f32[160,256]{1,0:T(8,128)S(1)}, f32[160,256]{1,0:T(8,128)S(1)}, u32[]{:S(2)}, u32[]{:S(2)}) %collective-permute-start.2) | collective-permute-done | bytes 163872 | tf_op jit(solution)/shard_map/ppermute | solution.py:218
  132.1 1.7 %collective-permute-done.7 = f32[160,256]{1,0:T(8,128)S(1)} collective-permute-done((f32[160,256]{1,0:T(8,128)S(1)}, f32[160,256]{1,0:T(8,128)S(1)}, u32[]{:S(2)}, u32[]{:S(2)}) %collective-permute-start.7) | collective-permute-done | bytes 163872 | tf_op jit(solution)/shard_map/ppermute | solution.py:218
  133.8 0.6 reduce_sum.12
  134.4 6.3 %collective-permute-done.3.mine_ref = f32[160,256]{1,0:T(8,128)S(1)} collective-permute-done((f32[160,256]{1,0:T(8,128)S(1)}, f32[160,256]{1,0:T(8,128)S(1)}, u32[]{:S(2)}, u32[]{:S(2)}) %collective-permute-start.3) | collective-permute-done | bytes 163872 | tf_op jit(solution)/shard_map/ppermute | solution.py:218
  140.7 0.7 shard_map.63
  (32 shorter events, 1.0 us)
Async XLA Ops:
  45.8 0.7 copy-start
  46.4 8.7 %collective-permute-start.4 = (f32[80,256]{1,0:T(8,128)S(1)}, f32[80,256]{1,0:T(8,128)S(1)}, u32[]{:S(2)}, u32[]{:S(2)}) collective-permute-start(f32[80,256]{1,0:T(8,128)S(1)} %get-tuple-element.20), channel_id=1, source_target_pairs={{0,16},{1,113},{16,32},{17,1},{32,48},{33,17},{48,64},{49,33},{64,... | collective-permute-start | bytes 245768 | tf_op jit(solution)/shard_map/ppermute | solution.py:218
  46.5 5.9 %collective-permute-start.9 = (s32[2,256]{1,0:T(2,128)S(1)}, s32[2,256]{1,0:T(2,128)S(1)}, u32[]{:S(2)}, u32[]{:S(2)}) collective-permute-start(s32[2,256]{1,0:T(2,128)S(1)} %copy-done), channel_id=1, source_target_pairs={{0,1},{1,0},{2,3},{3,2},{4,5},{5,4},{6,7},{7,6},{8,9},{9,8},{10,11... | collective-permute-start | bytes 6152 | tf_op jit(solution)/shard_map/ppermute | solution.py:222
  55.1 55.0 %collective-permute-start.5 = (f32[160,256]{1,0:T(8,128)S(1)}, f32[160,256]{1,0:T(8,128)S(1)}, u32[]{:S(2)}, u32[]{:S(2)}) collective-permute-start(f32[160,256]{1,0:T(8,128)S(1)} %shard_map.62), channel_id=1, source_target_pairs={{0,16},{1,113},{16,32},{17,1},{32,48},{33,17},{48,64},{49,33},{64,... | collective-permute-start | bytes 491528 | tf_op jit(solution)/shard_map/ppermute | solution.py:218
  55.3 11.9 %collective-permute-start.10 = (s32[8,128]{1,0:T(8,128)S(1)}, s32[8,128]{1,0:T(8,128)S(1)}, u32[]{:S(2)}, u32[]{:S(2)}) collective-permute-start(s32[8,128]{1,0:T(8,128)S(1)} %get-tuple-element.28), channel_id=1, source_target_pairs={{0,16},{16,32},{32,48},{48,64},{64,80},{80,96},{96,112},{112,0},{1... | collective-permute-start | bytes 12296 | tf_op jit(solution)/shard_map/ppermute | solution.py:209
  55.4 20.7 %collective-permute-start.11 = (s32[8,128]{1,0:T(8,128)S(1)}, s32[8,128]{1,0:T(8,128)S(1)}, u32[]{:S(2)}, u32[]{:S(2)}) collective-permute-start(s32[8,128]{1,0:T(8,128)S(1)} %get-tuple-element.27), channel_id=1, source_target_pairs={{0,32},{16,48},{32,64},{48,80},{64,96},{80,112},{96,0},{112,16},{1... | collective-permute-start | bytes 12296 | tf_op jit(solution)/shard_map/ppermute | solution.py:209
  59.3 20.1 %collective-permute-start.12 = (s32[8,128]{1,0:T(8,128)S(1)}, s32[8,128]{1,0:T(8,128)S(1)}, u32[]{:S(2)}, u32[]{:S(2)}) collective-permute-start(s32[8,128]{1,0:T(8,128)S(1)} %get-tuple-element.26), channel_id=1, source_target_pairs={{0,48},{16,64},{32,80},{48,96},{64,112},{80,0},{96,16},{112,32},{1... | collective-permute-start | bytes 12296 | tf_op jit(solution)/shard_map/ppermute | solution.py:209
  65.7 13.7 %collective-permute-start.13 = (s32[8,128]{1,0:T(8,128)S(1)}, s32[8,128]{1,0:T(8,128)S(1)}, u32[]{:S(2)}, u32[]{:S(2)}) collective-permute-start(s32[8,128]{1,0:T(8,128)S(1)} %get-tuple-element.25), channel_id=1, source_target_pairs={{0,64},{16,80},{32,96},{48,112},{64,0},{80,16},{96,32},{112,48},{1... | collective-permute-start | bytes 12296 | tf_op jit(solution)/shard_map/ppermute | solution.py:209
  67.2 12.2 %collective-permute-start.14 = (s32[8,128]{1,0:T(8,128)S(1)}, s32[8,128]{1,0:T(8,128)S(1)}, u32[]{:S(2)}, u32[]{:S(2)}) collective-permute-start(s32[8,128]{1,0:T(8,128)S(1)} %get-tuple-element.24), channel_id=1, source_target_pairs={{0,80},{16,96},{32,112},{48,0},{64,16},{80,32},{96,48},{112,64},{1... | collective-permute-start | bytes 12296 | tf_op jit(solution)/shard_map/ppermute | solution.py:209
  76.1 7.6 %collective-permute-start.15 = (s32[8,128]{1,0:T(8,128)S(1)}, s32[8,128]{1,0:T(8,128)S(1)}, u32[]{:S(2)}, u32[]{:S(2)}) collective-permute-start(s32[8,128]{1,0:T(8,128)S(1)} %get-tuple-element.23), channel_id=1, source_target_pairs={{0,96},{16,112},{32,0},{48,16},{64,32},{80,48},{96,64},{112,80},{1... | collective-permute-start | bytes 12296 | tf_op jit(solution)/shard_map/ppermute | solution.py:209
  79.4 4.5 %collective-permute-start.16 = (s32[8,128]{1,0:T(8,128)S(1)}, s32[8,128]{1,0:T(8,128)S(1)}, u32[]{:S(2)}, u32[]{:S(2)}) collective-permute-start(s32[8,128]{1,0:T(8,128)S(1)} %get-tuple-element.22), channel_id=1, source_target_pairs={{0,112},{16,0},{32,16},{48,32},{64,48},{80,64},{96,80},{112,96},{1... | collective-permute-start | bytes 12296 | tf_op jit(solution)/shard_map/ppermute | solution.py:209
  84.7 6.3 %collective-permute-start.17 = (f32[72,128]{1,0:T(8,128)S(1)}, f32[72,128]{1,0:T(8,128)S(1)}, u32[]{:S(2)}, u32[]{:S(2)}) collective-permute-start(f32[72,128]{1,0:T(8,128)S(1)} %shard_map.65.refs_8_), channel_id=1, source_target_pairs={{0,16},{1,113},{16,32},{17,1},{32,48},{33,17},{48,64},{49,33},{64,... | collective-permute-start | bytes 110600 | tf_op jit(solution)/shard_map/ppermute | solution.py:218
  91.0 6.1 %collective-permute-start.18 = (f32[72,128]{1,0:T(8,128)S(1)}, f32[72,128]{1,0:T(8,128)S(1)}, u32[]{:S(2)}, u32[]{:S(2)}) collective-permute-start(f32[72,128]{1,0:T(8,128)S(1)} %collective-permute-done.17.refs_0_), channel_id=1, source_target_pairs={{0,16},{1,113},{16,32},{17,1},{32,48},{33,17},{48,64},{49,33},{64,... | collective-permute-start | bytes 110600 | tf_op jit(solution)/shard_map/ppermute | solution.py:218
  91.0 18.9 %collective-permute-start = (f32[80,256]{1,0:T(8,128)S(1)}, f32[80,256]{1,0:T(8,128)S(1)}, u32[]{:S(2)}, u32[]{:S(2)}) collective-permute-start(f32[80,256]{1,0:T(8,128)S(1)} %get-tuple-element.16), channel_id=1, source_target_pairs={{0,16},{1,113},{16,32},{17,1},{32,48},{33,17},{48,64},{49,33},{64,... | collective-permute-start | bytes 245768 | tf_op jit(solution)/shard_map/ppermute | solution.py:218
  97.1 6.3 %collective-permute-start.19 = (f32[72,128]{1,0:T(8,128)S(1)}, f32[72,128]{1,0:T(8,128)S(1)}, u32[]{:S(2)}, u32[]{:S(2)}) collective-permute-start(f32[72,128]{1,0:T(8,128)S(1)} %collective-permute-done.18.refs_1_), channel_id=1, source_target_pairs={{0,16},{1,113},{16,32},{17,1},{32,48},{33,17},{48,64},{49,33},{64,... | collective-permute-start | bytes 110600 | tf_op jit(solution)/shard_map/ppermute | solution.py:218
  103.4 6.3 %collective-permute-start.20 = (f32[72,128]{1,0:T(8,128)S(1)}, f32[72,128]{1,0:T(8,128)S(1)}, u32[]{:S(2)}, u32[]{:S(2)}) collective-permute-start(f32[72,128]{1,0:T(8,128)S(1)} %collective-permute-done.19.refs_2_), channel_id=1, source_target_pairs={{0,16},{1,113},{16,32},{17,1},{32,48},{33,17},{48,64},{49,33},{64,... | collective-permute-start | bytes 110600 | tf_op jit(solution)/shard_map/ppermute | solution.py:218
  109.7 4.0 %collective-permute-start.21 = (f32[72,128]{1,0:T(8,128)S(1)}, f32[72,128]{1,0:T(8,128)S(1)}, u32[]{:S(2)}, u32[]{:S(2)}) collective-permute-start(f32[72,128]{1,0:T(8,128)S(1)} %shard_map.66.refs_9_), channel_id=1, source_target_pairs={{0,1},{1,0},{2,3},{3,2},{4,5},{5,4},{6,7},{7,6},{8,9},{9,8},{10,11... | collective-permute-start | bytes 110600 | tf_op jit(solution)/shard_map/ppermute | solution.py:222
  109.9 11.0 %collective-permute-start.1 = (f32[160,256]{1,0:T(8,128)S(1)}, f32[160,256]{1,0:T(8,128)S(1)}, u32[]{:S(2)}, u32[]{:S(2)}) collective-permute-start(f32[160,256]{1,0:T(8,128)S(1)} %shard_map.61), channel_id=1, source_target_pairs={{0,16},{1,113},{16,32},{17,1},{32,48},{33,17},{48,64},{49,33},{64,... | collective-permute-start | bytes 491528 | tf_op jit(solution)/shard_map/ppermute | solution.py:218
  110.1 12.3 %collective-permute-start.6 = (f32[160,256]{1,0:T(8,128)S(1)}, f32[160,256]{1,0:T(8,128)S(1)}, u32[]{:S(2)}, u32[]{:S(2)}) collective-permute-start(f32[160,256]{1,0:T(8,128)S(1)} %add.85), channel_id=1, source_target_pairs={{0,16},{1,113},{16,32},{17,1},{32,48},{33,17},{48,64},{49,33},{64,... | collective-permute-start | bytes 491528 | tf_op jit(solution)/shard_map/ppermute | solution.py:218
  115.2 18.6 %all-to-all-start.1 = ((bf16[8,32,256]{2,1,0:T(8,128)(2,1)}), bf16[8,32,256]{2,1,0:T(8,128)(2,1)S(1)}, u32[]{:S(2)}, u32[]{:S(2)}) async-start(bf16[8,32,256]{2,1,0:T(8,128)(2,1)} %bitcast.11), calls=%async_computation.1 | async-start | bytes 262144 | tf_op jit(solution)/shard_map/all_to_all | solution.py:205
  121.0 11.0 %collective-permute-start.2 = (f32[160,256]{1,0:T(8,128)S(1)}, f32[160,256]{1,0:T(8,128)S(1)}, u32[]{:S(2)}, u32[]{:S(2)}) collective-permute-start(f32[160,256]{1,0:T(8,128)S(1)} %add.83), channel_id=1, source_target_pairs={{0,16},{1,113},{16,32},{17,1},{32,48},{33,17},{48,64},{49,33},{64,... | collective-permute-start | bytes 491528 | tf_op jit(solution)/shard_map/ppermute | solution.py:218
  122.4 11.4 %collective-permute-start.7 = (f32[160,256]{1,0:T(8,128)S(1)}, f32[160,256]{1,0:T(8,128)S(1)}, u32[]{:S(2)}, u32[]{:S(2)}) collective-permute-start(f32[160,256]{1,0:T(8,128)S(1)} %add.86), channel_id=1, source_target_pairs={{0,16},{1,113},{16,32},{17,1},{32,48},{33,17},{48,64},{49,33},{64,... | collective-permute-start | bytes 491528 | tf_op jit(solution)/shard_map/ppermute | solution.py:218
  132.0 8.7 %collective-permute-start.3 = (f32[160,256]{1,0:T(8,128)S(1)}, f32[160,256]{1,0:T(8,128)S(1)}, u32[]{:S(2)}, u32[]{:S(2)}) collective-permute-start(f32[160,256]{1,0:T(8,128)S(1)} %add.84), channel_id=1, source_target_pairs={{0,16},{1,113},{16,32},{17,1},{32,48},{33,17},{48,64},{49,33},{64,... | collective-permute-start | bytes 491528 | tf_op jit(solution)/shard_map/ppermute | solution.py:218
  133.8 6.9 %collective-permute-start.8 = (f32[160,256]{1,0:T(8,128)S(1)}, f32[160,256]{1,0:T(8,128)S(1)}, u32[]{:S(2)}, u32[]{:S(2)}) collective-permute-start(f32[160,256]{1,0:T(8,128)S(1)} %collective-permute-done.7), channel_id=1, source_target_pairs={{0,1},{1,0},{2,3},{3,2},{4,5},{5,4},{6,7},{7,6},{8,9},{9,8},{10,11... | collective-permute-start | bytes 491528 | tf_op jit(solution)/shard_map/ppermute | solution.py:222
